TPU v7x, 32 devices: a whole 2x2x4 slice. The times are simulated.
32 devices in a mesh: grp: 2 (over y), bank: 4 (over z), seg: 4 (over x, core).
Axes of the slice: x: 2, y: 2, z: 4, core: 2. Of those that a mesh axis runs over, the one named last changes fastest.
Arguments:
- strain: bfloat16 [32, 2, 32768], P(('grp', 'seg'), None, 'bank'), parts along dimension 0, may hold values from -6 to 6
- templates: bfloat16 [4, 2, 32768], P('bank'), may hold values from -6 to 6
- length_bins: int32 [4], P('bank'), may hold values from 0 to 3
Outputs:
- snr_table: float32 [4, 32], P('bank', ('grp', 'seg')), parts along dimension 1
- segment_peak: float32 [32], P(('grp', 'seg')), parts along dimension 0
- template_peak: float32 [8], P(('grp', 'bank')), parts along dimension 0
There are 2 independent parts, one for each index of `grp`. A program takes and returns all parts, laid end to end along the dimension named above; an argument that names none is the same for every part. Nothing has to cross between parts.
All inputs are finite; a program needn't handle non-finite values.
Results may differ from a plain program's by a relative error of at most 0.0003.
Values may be sent and summed in bfloat16 or wider, within the bound.
A program may use at most 64 MiB of HBM per device.

v0:
```python
import functools
import math

import jax
import jax.numpy as jnp
import numpy as np
from jax import lax
from jax.experimental import pallas as pl
from jax.experimental.pallas import tpu as pltpu
from jax.sharding import PartitionSpec as P

MESH = pl.DeviceIdType.MESH
EPSILON = 1e-06
LANES = 128


def split(value):
    high = value.astype(jnp.bfloat16)
    low = (value - high.astype(jnp.float32)).astype(jnp.bfloat16)
    return high, low


def tables(length):
    rows = length // LANES
    half = rows // 2

    def root(phase, period):
        angle = 2.0 * math.pi * (phase % period) / period
        return np.cos(angle), np.sin(angle)

    r = np.arange(half)
    c = np.arange(LANES)
    row_c, row_s = root(np.outer(r, r), half)
    first = np.block([[row_c, -row_s], [row_s, row_c]])
    col_c, col_s = root(np.outer(c, c), LANES)
    last = np.block([[col_c, col_s], [-col_s, col_c]])
    odd = np.stack([np.broadcast_to(part[:, None], (half, LANES)) for part in root(r, rows)])
    turn = [root(np.outer(2 * r + p, c), length) for p in (0, 1)]
    turn = np.stack([np.concatenate([turn[0][i], turn[1][i]], axis=1) for i in (0, 1)])

    def halves(matrix):
        high = matrix.astype(jnp.bfloat16)
        low = (matrix - high.astype(np.float64)).astype(jnp.bfloat16)
        return high, low

    f_high, f_low = halves(first)
    l_high, l_low = halves(last)
    first = np.concatenate([f_high, f_high, f_low], axis=1)
    last = np.concatenate([l_high, l_high, l_low], axis=0)
    return first, last, odd.astype(np.float32), turn.astype(np.float32)


def kernel(
    banks, segs, chunks, give,
    strain_hbm, tpl_hbm, bins_ref, first_hbm, last_hbm, odd_hbm, turn_hbm,
    out_ref,
    strain_ref, tpl_ref, masked, lent, held, tpl_re, tpl_im, two_re, two_im, work, first, last, odd, turn,
    row_bank, row_seg, row_far,
    input_sem, table_sem, right_sem, left_sem, recv_sem, bank_send, bank_recv, seg_send, seg_recv,
    far_send, far_recv, tpl_send, tpl_recv,
):
    me = lax.axis_index("bank")
    my_seg = lax.axis_index("seg")
    count, depth, _ = strain_ref.shape
    size = count // chunks
    rows = tpl_ref.shape[0] // 2
    half = rows // 2

    def part(chunk):
        return pl.ds(chunk * size, size)

    barrier = pltpu.get_barrier_semaphore()
    has_left, has_right = me > 0, me < banks - 1
    is_end = jnp.logical_not(has_left & has_right) & (give > 0)
    helps = ((me == 1) | (me == banks - 2)) & (give > 0)
    helper = jnp.where(me == 0, 1, banks - 2)
    helped = jnp.where(me == 1, 0, banks - 1)

    def wanted(device, chunk):
        least = 1 if chunk >= chunks - give else 0
        return (device >= least) & (device < banks - least)


    @pl.when(has_left)
    def _():
        pl.semaphore_signal(barrier, inc=1, device_id={"bank": me - 1}, device_id_type=MESH)

    @pl.when(has_right)
    def _():
        pl.semaphore_signal(barrier, inc=1, device_id={"bank": me + 1}, device_id_type=MESH)

    for step in range(1, segs):
        pl.semaphore_signal(
            barrier, inc=1, device_id={"seg": lax.rem(my_seg + step, segs)}, device_id_type=MESH
        )
    if give:
        for step in range(1, segs):
            @pl.when(is_end)
            def _():
                pl.semaphore_signal(
                    barrier, inc=1, device_id={"bank": helper, "seg": lax.rem(my_seg + step, segs)},
                    device_id_type=MESH,
                )

    inputs = [
        pltpu.make_async_copy(source, target, input_sem.at[i])
        for i, (source, target) in enumerate(
            [(strain_hbm.at[part(chunk)], strain_ref.at[part(chunk)]) for chunk in range(chunks)]
            + [(tpl_hbm, tpl_ref)]
        )
    ]
    for load in inputs:
        load.start()
    loads = [
        pltpu.make_async_copy(source, target, table_sem.at[i])
        for i, (source, target) in enumerate(
            ((first_hbm, first), (odd_hbm, odd), (turn_hbm, turn), (last_hbm, last))
        )
    ]
    for load in loads:
        load.start()
    pl.semaphore_wait(barrier, has_left.astype(jnp.int32) + has_right.astype(jnp.int32) + segs - 1 + helps.astype(jnp.int32) * (segs - 1))

    def move(source, origin, chunk, step):
        sems = right_sem if step > 0 else left_sem
        return pltpu.make_async_remote_copy(
            src_ref=source,
            dst_ref=held.at[origin, part(chunk)],
            send_sem=sems.at[origin, chunk],
            recv_sem=recv_sem.at[origin, chunk],
            device_id={"bank": me + step},
            device_id_type=MESH,
        )

    for chunk in range(chunks):
        inputs[chunk].wait()

        @pl.when(wanted(me + 1, chunk))
        def _():
            move(strain_ref.at[part(chunk)], me, chunk, 1).start()

        @pl.when(wanted(me - 1, chunk))
        def _():
            move(strain_ref.at[part(chunk)], me, chunk, -1).start()

    held[me] = strain_ref[...]

    for load in inputs[chunks:]:
        load.wait()
    position = lax.broadcasted_iota(jnp.int32, (2 * rows, LANES), 0) // 2 * LANES
    position = position + lax.broadcasted_iota(jnp.int32, (2 * rows, LANES), 1)
    keep = position < lax.shift_right_logical(jnp.full((1, 1), rows * LANES, jnp.int32), bins_ref[...])
    value = jnp.where(keep, tpl_ref[...].astype(jnp.float32), 0.0)
    if give:
        masked[...] = value.astype(jnp.bfloat16)

    def prepare(interleaved, re_ref, im_ref):
        work[...] = interleaved
        re_ref[...] = work[pl.ds(0, rows, stride=2), :]
        im_ref[...] = work[pl.ds(1, rows, stride=2), :]
        return jnp.sqrt(jnp.sum(interleaved * interleaved, keepdims=True) + EPSILON)

    sigma = prepare(value, tpl_re, tpl_im)

    def lend():
        return pltpu.make_async_remote_copy(
            src_ref=masked, dst_ref=lent, send_sem=tpl_send.at[0], recv_sem=tpl_recv.at[0],
            device_id={"bank": helper}, device_id_type=MESH,
        )

    if give:
        @pl.when(is_end)
        def _():
            lend().start()

    for load in loads:
        load.wait()

    def peak(seg, re_ref, im_ref):
        work[...] = held[:, seg].reshape(2 * rows, LANES).astype(jnp.float32)
        s_re = work[pl.ds(0, rows, stride=2), :]
        s_im = work[pl.ds(1, rows, stride=2), :]
        h_re, h_im = re_ref[...], im_ref[...]
        q_re = h_re * s_re + h_im * s_im
        q_im = h_re * s_im - h_im * s_re
        even_re, even_im = q_re[:half] + q_re[half:], q_im[:half] + q_im[half:]
        d_re, d_im = q_re[:half] - q_re[half:], q_im[:half] - q_im[half:]
        odd_re = d_re * odd[0] - d_im * odd[1]
        odd_im = d_re * odd[1] + d_im * odd[0]
        y = jnp.concatenate(
            [
                jnp.concatenate([even_re, odd_re], axis=1),
                jnp.concatenate([even_im, odd_im], axis=1),
            ],
            axis=0,
        )
        high, low = split(y)
        u = jnp.dot(
            first[...],
            jnp.concatenate([high, low, high], axis=0),
            preferred_element_type=jnp.float32,
        )
        u_re, u_im = u[:half], u[half:]
        v_re = u_re * turn[0] - u_im * turn[1]
        v_im = u_re * turn[1] + u_im * turn[0]
        x = jnp.concatenate(
            [
                jnp.concatenate([v_re[:, :LANES], v_im[:, :LANES]], axis=1),
                jnp.concatenate([v_re[:, LANES:], v_im[:, LANES:]], axis=1),
            ],
            axis=0,
        )
        high, low = split(x)
        z = jnp.dot(
            jnp.concatenate([high, low, high], axis=1),
            last[...],
            preferred_element_type=jnp.float32,
        )
        z_re, z_im = z[:, :LANES], z[:, LANES:]
        power = z_re * z_re + z_im * z_im
        return jnp.max(power, keepdims=True)

    lane = lax.broadcasted_iota(jnp.int32, (8, LANES), 1)
    line = lax.broadcasted_iota(jnp.int32, (8, LANES), 0)
    row_bank[me] = jnp.zeros((8, LANES), jnp.float32)

    def note(seg, which, snr):
        row_bank[me] = jnp.where((lane == seg) & (line == which), snr, row_bank[me])

    for distance in range(1, banks):
        for chunk in range(chunks):
            for step in (1, -1):
                origin = me - step * distance
                inside = (origin >= 0) & (origin < banks) & wanted(me, chunk)

                @pl.when(inside)
                def _():
                    block = held.at[origin, part(chunk)]
                    move(block, origin, chunk, step).wait_recv()

                    @pl.when(wanted(me + step, chunk))
                    def _():
                        move(block, origin, chunk, step).start()

            if distance == banks - 1:
                for seg in range(chunk * size, (chunk + 1) * size):
                    if chunk < chunks - give:
                        note(seg, 0, jnp.sqrt(peak(seg, tpl_re, tpl_im)) / sigma)
                        continue

                    @pl.when(helps)
                    def _():
                        if chunk == chunks - give:
                            lend().wait_recv()
                        sigma_two = prepare(lent[...].astype(jnp.float32), two_re, two_im)
                        one = peak(seg, tpl_re, tpl_im)
                        two = peak(seg, two_re, two_im)
                        note(seg, 0, jnp.sqrt(one) / sigma)
                        note(seg, 1, jnp.sqrt(two) / sigma_two)

    row_seg[my_seg] = row_bank[me]

    def tell(buffer, axis, index, peer, send, recv):
        return pltpu.make_async_remote_copy(
            src_ref=buffer.at[index],
            dst_ref=buffer.at[index],
            send_sem=send.at[peer],
            recv_sem=recv.at[index],
            device_id={axis: peer},
            device_id_type=MESH,
        )

    def far(peer):
        return pltpu.make_async_remote_copy(
            src_ref=row_seg.at[my_seg], dst_ref=row_far.at[my_seg],
            send_sem=far_send.at[peer], recv_sem=far_recv.at[my_seg],
            device_id={"bank": helped, "seg": peer}, device_id_type=MESH,
        )

    def heard(peer):
        return pltpu.make_async_remote_copy(
            src_ref=row_seg.at[my_seg], dst_ref=row_far.at[peer],
            send_sem=far_send.at[peer], recv_sem=far_recv.at[peer],
            device_id={"bank": helper, "seg": peer}, device_id_type=MESH,
        )

    groups = (
        (row_bank, "bank", me, banks, bank_send, bank_recv),
        (row_seg, "seg", my_seg, segs, seg_send, seg_recv),
    )
    for buffer, axis, index, number, send, recv in groups:
        for step in range(1, number):
            tell(buffer, axis, index, lax.rem(index + step, number), send, recv).start()
    peers = [lax.rem(my_seg + step, segs) for step in range(1, segs)]
    if give:
        @pl.when(helps)
        def _():
            for peer in peers:
                far(peer).start()
    for chunk in range(chunks):
        for step, sems in ((1, right_sem), (-1, left_sem)):
            for distance in range(banks):
                origin = me - step * distance

                @pl.when((origin >= 0) & (origin < banks) & wanted(me + step, chunk))
                def _():
                    move(held.at[origin, part(chunk)], origin, chunk, step).wait_send()

    for buffer, axis, index, number, send, recv in reversed(groups):
        for step in range(1, number):
            other = lax.rem(index + step, number)
            tell(buffer, axis, other, other, send, recv).wait_recv()
    segment_peak = jnp.max(row_bank[...], axis=(0, 1))[None, :]
    table = row_bank[me][:1]
    template_row = jnp.max(row_seg[...], axis=0)[:1]

    def give_out(table, template_row):
        template_peak = jnp.max(template_row, axis=1, keepdims=True)
        out_ref[...] = jnp.where(line == 0, table, jnp.where(line == 1, segment_peak, template_peak))

    if give:
        @pl.when(is_end)
        def _():
            theirs = row_bank[helper][1:2]
            every = jnp.maximum(template_row, theirs)
            for peer in peers:
                heard(peer).wait_recv()
                every = jnp.maximum(every, row_far[peer][1:2])
            give_out(jnp.maximum(table, theirs), every)

        @pl.when(jnp.logical_not(is_end))
        def _():
            give_out(table, template_row)

        @pl.when(is_end)
        def _():
            lend().wait_send()

        @pl.when(helps)
        def _():
            for peer in peers:
                far(peer).wait_send()
    else:
        give_out(table, template_row)
    for buffer, axis, index, number, send, recv in groups:
        for step in range(1, number):
            tell(buffer, axis, index, lax.rem(index + step, number), send, recv).wait_send()


def unpack(out_ref, table_ref, segment_ref, template_ref):
    table_ref[...] = out_ref[0:1, : table_ref.shape[1]]
    segment_ref[...] = out_ref[1, : segment_ref.shape[0]]
    template_ref[...] = out_ref[2, :1]


def per_device(banks, segs, strain, templates, length_bins):
    count, _, width = strain.shape
    length = templates.shape[2]
    depth, rows = width // LANES, length // LANES
    chunks = count if banks <= 8 else 1
    give = 1 if banks == 4 and chunks == count > 1 else 0
    first, last, odd, turn = tables(length)
    strain = strain.reshape(count, 2, depth, LANES).transpose(0, 2, 1, 3).reshape(count, 2 * depth, LANES)
    tpl = templates.reshape(2, rows, LANES).transpose(1, 0, 2).reshape(2 * rows, LANES)
    vmem = pl.BlockSpec(memory_space=pltpu.VMEM)
    hbm = pl.BlockSpec(memory_space=pltpu.HBM)
    dma = pltpu.SemaphoreType.DMA
    out = pl.pallas_call(
        functools.partial(kernel, banks, segs, chunks, give),
        out_shape=jax.ShapeDtypeStruct((8, LANES), jnp.float32),
        in_specs=[hbm, hbm, vmem, hbm, hbm, hbm, hbm],
        out_specs=vmem,
        scratch_shapes=[
            pltpu.VMEM(strain.shape, strain.dtype),
            pltpu.VMEM(tpl.shape, tpl.dtype),
            pltpu.VMEM(tpl.shape, tpl.dtype),
            pltpu.VMEM(tpl.shape, tpl.dtype),
            pltpu.VMEM((banks, count, 2 * depth, LANES), jnp.bfloat16),
            pltpu.VMEM((rows, LANES), jnp.float32),
            pltpu.VMEM((rows, LANES), jnp.float32),
            pltpu.VMEM((rows, LANES), jnp.float32),
            pltpu.VMEM((rows, LANES), jnp.float32),
            pltpu.VMEM((2 * rows, LANES), jnp.float32),
            pltpu.VMEM(first.shape, first.dtype),
            pltpu.VMEM(last.shape, last.dtype),
            pltpu.VMEM(odd.shape, odd.dtype),
            pltpu.VMEM(turn.shape, turn.dtype),
            pltpu.VMEM((banks, 8, LANES), jnp.float32),
            pltpu.VMEM((segs, 8, LANES), jnp.float32),
            pltpu.VMEM((segs, 8, LANES), jnp.float32),
            dma((chunks + 1,)),
            dma((4,)),
            dma((banks, chunks)),
            dma((banks, chunks)),
            dma((banks, chunks)),
            dma((banks,)),
            dma((banks,)),
            dma((segs,)),
            dma((segs,)),
            dma((segs,)),
            dma((segs,)),
            dma((1,)),
            dma((1,)),
        ],
        compiler_params=pltpu.CompilerParams(collective_id=0, has_side_effects=True),
        name="search",
    )(strain, tpl, length_bins.reshape(1, 1), first, last, odd, turn)
    return pl.pallas_call(
        unpack,
        out_shape=[
            jax.ShapeDtypeStruct((1, count), jnp.float32),
            jax.ShapeDtypeStruct((count,), jnp.float32),
            jax.ShapeDtypeStruct((1,), jnp.float32),
        ],
        in_specs=[vmem],
        out_specs=[vmem] * 3,
        name="unpack",
    )(out)


def solution(mesh):
    placed = (P(("grp", "seg"), None, "bank"), P("bank", None, None), P("bank"))
    return jax.shard_map(
        functools.partial(per_device, mesh.shape["bank"], mesh.shape["seg"]),
        mesh=mesh,
        in_specs=placed,
        out_specs=(P("bank", ("grp", "seg")), P(("grp", "seg")), P(("grp", "bank"))),
        check_vma=False,
    )
```

profile of v0, /device:TPU:0, one launch (start us, length us, event | category | flops | bytes accessed | tf_op | source)
XLA Modules:
  0.0 23.6 jit_solution(12048898122537391838)
XLA Ops:
  1.3 21.1 %search.1.out_ref = f32[8,128]{1,0:T(8,128)} custom-call(bf16[4,128,128]{2,1,0:T(8,128)(2,1)} %bitcast.12, bf16[512,128]{1,0:T(8,128)(2,1)} %bitcast.13, s32[1,1]{1,0:T(1,128)} %bitcast.11.bins_ref, bf16[256,768]{1,0:T(8,128)(2,1)} %constant.8.clone.first_hbm, bf16[768,256]{1,0:T(8,128)(2,1)} %constant.9.clone.last_hbm, ...), custom_call_target="tpu_custom_call" | custom-call | tf_op jit(solution)/shard_map/search/pallas_call | solution.py:368
  22.3 1.2 %unpack.1 = (f32[1,4]{1,0:T(1,128)}, f32[4]{0:T(128)}, f32[1]{0:T(128)}) custom-call(f32[8,128]{1,0:T(8,128)} %search.1.out_ref), custom_call_target="tpu_custom_call" | custom-call | tf_op jit(solution)/shard_map/unpack/pallas_call | solution.py:408
where the time goes:
time: 23.7 us; the launch traced here: 23.6 us
  Pallas kernels  22.3 us (94%)
  between operations  1.28 us (5%)
    pallas_call x1, Pallas kernels, per_device(): pl.pallas_call(functools.partial(kernel, banks, segs, chunks, give), out_...  21.1 us
    pallas_call x1, Pallas kernels, per_device(): pl.pallas_call(unpack, out_shape=[jax.ShapeDtypeStruct((1, count), jnp.fl...  1.2 us

commit v1 on v0

--- a/solution.py
+++ b/solution.py
@@ -12,6 +12,7 @@
 MESH = pl.DeviceIdType.MESH
 EPSILON = 1e-06
 LANES = 128
+GRANT = 56492032
 
 
 def split(value):
@@ -402,7 +403,7 @@
             dma((1,)),
             dma((1,)),
         ],
-        compiler_params=pltpu.CompilerParams(collective_id=0, has_side_effects=True),
+        compiler_params=pltpu.CompilerParams(collective_id=0, has_side_effects=True, vmem_limit_bytes=GRANT),
         name="search",
     )(strain, tpl, length_bins.reshape(1, 1), first, last, odd, turn)
     return pl.pallas_call(
@@ -412,6 +413,7 @@
             jax.ShapeDtypeStruct((count,), jnp.float32),
             jax.ShapeDtypeStruct((1,), jnp.float32),
         ],
+        compiler_params=pltpu.CompilerParams(vmem_limit_bytes=1 << 20),
         in_specs=[vmem],
         out_specs=[vmem] * 3,
         name="unpack",

time: 23.7 us -> 22.4 us (0.945)
  Pallas kernels: 22.3 us -> 21 us
    pallas_call x1, Pallas kernels: 1.2 us -> 0.52 us  [per_device(): pl.pallas_call(unpack, out_shape=[jax.ShapeDtypeStruct((1, count), jnp.fl...]
    pallas_call x1, Pallas kernels: 21.1 us -> 20.5 us  [per_device(): pl.pallas_call(functools.partial(kernel, banks, segs, chunks, give), out_...]
where the time goes in v1:
time: 22.4 us; the launch traced here: 22.3 us
  Pallas kernels  21 us (94%)
  between operations  1.28 us (6%)
    pallas_call x1, Pallas kernels, per_device(): pl.pallas_call(functools.partial(kernel, banks, segs, chunks, give), out_...  20.5 us
    pallas_call x1, Pallas kernels, per_device(): pl.pallas_call(unpack, out_shape=[jax.ShapeDtypeStruct((1, count), jnp.fl...  0.52 us

profile of v1, /device:TPU:0, one launch (start us, length us, event | category | flops | bytes accessed | tf_op | source)
XLA Modules:
  0.0 22.3 jit_solution(13460720451459082381)
XLA Ops:
  1.3 20.5 %search.1.out_ref = f32[8,128]{1,0:T(8,128)S(1)} custom-call(bf16[4,128,128]{2,1,0:T(8,128)(2,1)} %bitcast.12, bf16[512,128]{1,0:T(8,128)(2,1)} %bitcast.13, s32[1,1]{1,0:T(1,128)} %bitcast.11.bins_ref, bf16[256,768]{1,0:T(8,128)(2,1)} %constant.8.clone.first_hbm, bf16[768,256]{1,0:T(8,128)(2,1)} %constant.9.clone.last_hbm, ...), custom_call_target="tpu_custom_call" | custom-call | tf_op jit(solution)/shard_map/search/pallas_call | solution.py:369
  21.8 0.5 %unpack.1 = (f32[1,4]{1,0:T(1,128)}, f32[4]{0:T(128)}, f32[1]{0:T(128)}) custom-call(f32[8,128]{1,0:T(8,128)S(1)} %search.1.out_ref), custom_call_target="tpu_custom_call" | custom-call | tf_op jit(solution)/shard_map/unpack/pallas_call | solution.py:409

commit v2 on v1

v2 whole, which is shorter than its diff:
```python
import functools
import math

import jax
import jax.numpy as jnp
import numpy as np
from jax import lax
from jax.experimental import pallas as pl
from jax.experimental.pallas import tpu as pltpu
from jax.sharding import PartitionSpec as P

MESH = pl.DeviceIdType.MESH
EPSILON = 1e-06
LANES = 128
GRANT = 56492032


def split(value):
    high = value.astype(jnp.bfloat16)
    low = (value - high.astype(jnp.float32)).astype(jnp.bfloat16)
    return high, low


def tables(length):
    rows = length // LANES
    half = rows // 2

    def root(phase, period):
        angle = 2.0 * math.pi * (phase % period) / period
        return np.cos(angle), np.sin(angle)

    r = np.arange(half)
    c = np.arange(LANES)
    row_c, row_s = root(np.outer(r, r), half)
    first = np.block([[row_c, -row_s], [row_s, row_c]])
    col_c, col_s = root(np.outer(c, c), LANES)
    last = np.block([[col_c, col_s], [-col_s, col_c]])
    odd = np.stack([np.broadcast_to(part[:, None], (half, LANES)) for part in root(r, rows)])
    turn = [root(np.outer(2 * r + p, c), length) for p in (0, 1)]
    turn = np.stack([np.concatenate([turn[0][i], turn[1][i]], axis=1) for i in (0, 1)])

    def halves(matrix):
        high = matrix.astype(jnp.bfloat16)
        low = (matrix - high.astype(np.float64)).astype(jnp.bfloat16)
        return high, low

    f_high, f_low = halves(first)
    l_high, l_low = halves(last)
    first = np.concatenate([f_high, f_high, f_low], axis=1)
    last = np.concatenate([l_high, l_high, l_low], axis=0)
    return first, last, odd.astype(np.float32), turn.astype(np.float32)


def transform(products, first, last, odd, turn):
    half = products[0][0].shape[0] // 2
    many = len(products)
    columns = []
    for q_re, q_im in products:
        even_re, even_im = q_re[:half] + q_re[half:], q_im[:half] + q_im[half:]
        d_re, d_im = q_re[:half] - q_re[half:], q_im[:half] - q_im[half:]
        odd_re = d_re * odd[0] - d_im * odd[1]
        odd_im = d_re * odd[1] + d_im * odd[0]
        columns.append(
            jnp.concatenate(
                [jnp.concatenate([even_re, odd_re], axis=1), jnp.concatenate([even_im, odd_im], axis=1)], axis=0
            )
        )
    high, low = split(jnp.concatenate(columns, axis=1))
    u = jnp.dot(first[...], jnp.concatenate([high, low, high], axis=0), preferred_element_type=jnp.float32)
    lines = []
    for i in range(many):
        part = u[:, 2 * LANES * i : 2 * LANES * (i + 1)]
        u_re, u_im = part[:half], part[half:]
        v_re = u_re * turn[0] - u_im * turn[1]
        v_im = u_re * turn[1] + u_im * turn[0]
        lines.append(jnp.concatenate([v_re[:, :LANES], v_im[:, :LANES]], axis=1))
        lines.append(jnp.concatenate([v_re[:, LANES:], v_im[:, LANES:]], axis=1))
    high, low = split(jnp.concatenate(lines, axis=0))
    z = jnp.dot(jnp.concatenate([high, low, high], axis=1), last[...], preferred_element_type=jnp.float32)
    z_re, z_im = z[:, :LANES], z[:, LANES:]
    power = z_re * z_re + z_im * z_im
    return [jnp.max(power[2 * half * i : 2 * half * (i + 1)], keepdims=True) for i in range(many)]


def middle(
    banks, segs,
    strain_hbm, tpl_hbm, bins_ref, first_hbm, last_hbm, odd_hbm, turn_hbm,
    out_ref,
    strain_ref, tpl_ref, masked, lent, held, h_re, h_im, s_re, s_im, work, first, last, odd, turn,
    mine, near, side, across,
    strain_sem, input_sem, table_sem, end_send, own_send, pass_send, block_recv, lend_send, lend_recv,
    near_send, near_recv, side_send, side_recv, across_send, across_recv, ready,
):
    me = lax.axis_index("bank")
    my_seg = lax.axis_index("seg")
    count = strain_ref.shape[0]
    rows = tpl_ref.shape[0] // 2
    is_end = (me == 0) | (me == banks - 1)
    is_hub = jnp.logical_not(is_end)
    hub = jnp.where(me == 0, 1, banks - 2)
    other = banks - 1 - me
    end = jnp.where(me == 1, 0, banks - 1)
    far_end = banks - 1 - end
    aside = [lax.rem(my_seg + step, segs) for step in range(1, segs)]

    barrier = pltpu.get_barrier_semaphore()

    def signal(semaphore, place):
        pl.semaphore_signal(semaphore, inc=1, device_id=place, device_id_type=MESH)

    @pl.when(is_end)
    def _():
        signal(barrier, {"bank": hub})

    @pl.when(is_hub)
    def _():
        signal(barrier, {"bank": other})
        signal(barrier, {"bank": end})
        for seg in aside:
            signal(barrier, {"seg": seg})

    blocks = [
        pltpu.make_async_copy(strain_hbm.at[chunk], strain_ref.at[chunk], strain_sem.at[chunk])
        for chunk in range(count)
    ]
    template = pltpu.make_async_copy(tpl_hbm, tpl_ref, input_sem.at[0])
    loads = [
        pltpu.make_async_copy(source, target, table_sem.at[i])
        for i, (source, target) in enumerate(((first_hbm, first), (odd_hbm, odd), (turn_hbm, turn), (last_hbm, last)))
    ]
    for load in blocks + [template]:
        load.start()

    @pl.when(is_hub)
    def _():
        for load in loads:
            load.start()

    def block_copy(source, origin, chunk, to, send):
        return pltpu.make_async_remote_copy(
            src_ref=source, dst_ref=held.at[origin, chunk],
            send_sem=send.at[chunk], recv_sem=block_recv.at[origin, chunk],
            device_id={"bank": to}, device_id_type=MESH,
        )

    def lend(to):
        return pltpu.make_async_remote_copy(
            src_ref=masked, dst_ref=lent, send_sem=lend_send.at[0], recv_sem=lend_recv.at[0],
            device_id={"bank": to}, device_id_type=MESH,
        )

    def near_copy(to):
        return pltpu.make_async_remote_copy(
            src_ref=mine.at[pl.ds(0, 3)], dst_ref=near, send_sem=near_send.at[0], recv_sem=near_recv.at[0],
            device_id={"bank": to}, device_id_type=MESH,
        )

    def side_copy(row, origin, bank, to):
        return pltpu.make_async_remote_copy(
            src_ref=mine.at[row], dst_ref=side.at[origin],
            send_sem=side_send.at[row // 3, to], recv_sem=side_recv.at[origin],
            device_id={"bank": bank, "seg": to}, device_id_type=MESH,
        )

    def across_copy(which, to):
        return pltpu.make_async_remote_copy(
            src_ref=mine.at[1], dst_ref=across, send_sem=across_send.at[which], recv_sem=across_recv.at[0],
            device_id={"bank": to}, device_id_type=MESH,
        )

    def masked_template():
        value = tpl_ref[...].astype(jnp.float32)
        position = lax.broadcasted_iota(jnp.int32, value.shape, 0) // 2 * LANES
        position = position + lax.broadcasted_iota(jnp.int32, value.shape, 1)
        cutoff = lax.shift_right_logical(jnp.full((1, 1), rows * LANES, jnp.int32), bins_ref[...])
        return jnp.where(position < cutoff, value, 0.0)

    def give_out(table, segment_peak, template_peak):
        line = lax.broadcasted_iota(jnp.int32, (8, LANES), 0)
        out_ref[...] = jnp.where(line == 0, table, jnp.where(line == 1, segment_peak, template_peak))

    @pl.when(is_end)
    def _():
        template.wait()
        masked[...] = masked_template().astype(jnp.bfloat16)
        pl.semaphore_wait(barrier, 1)
        for chunk in range(count):
            blocks[chunk].wait()
            block_copy(strain_ref.at[chunk], me, chunk, hub, end_send).start()
        lend(hub).start()
        for chunk in range(count):
            block_copy(strain_ref.at[chunk], me, chunk, hub, end_send).wait_send()
        lend(hub).wait_send()
        for seg in aside:
            side_copy(2, seg, me, my_seg).wait_recv()
        near_copy(me).wait_recv()
        across_copy(0, me).wait_recv()
        template_peak = near[2]
        for seg in aside:
            template_peak = jnp.maximum(template_peak, side[seg])
        give_out(near[0], jnp.maximum(near[1], across[...]), template_peak)

    def deinterleave(value, slot):
        work[slot] = value
        return work[slot, pl.ds(0, rows, stride=2), :], work[slot, pl.ds(1, rows, stride=2), :]

    def prepare(slot, value):
        h_re[slot], h_im[slot] = deinterleave(value, 2)
        return jnp.sqrt(jnp.sum(value * value, keepdims=True) + EPSILON)

    def product(slot, seg):
        a, b, c, d = s_re[seg], s_im[seg], h_re[slot], h_im[slot]
        return c * a + d * b, c * b - d * a

    def peaks(*pairs):
        return [jnp.sqrt(power) for power in transform([product(*pair) for pair in pairs], first, last, odd, turn)]

    @pl.when(is_hub)
    def _():
        pl.semaphore_wait(barrier, 2 + len(aside))
        for chunk in range(count):
            blocks[chunk].wait()
            block_copy(strain_ref.at[chunk], me, chunk, other, own_send).start()
        for seg in aside:
            signal(ready, {"seg": seg})
        template.wait()
        sigma = prepare(0, masked_template())
        for chunk in range(count):
            held[me, chunk] = strain_ref[chunk]
        for load in loads:
            load.wait()
        for chunk in range(count):
            block = held.at[end, chunk]
            block_copy(block, end, chunk, me, pass_send).wait_recv()
            block_copy(block, end, chunk, other, pass_send).start()

        def gather(chunk):
            for origin in (other, far_end):
                block_copy(held.at[origin, chunk], origin, chunk, me, pass_send).wait_recv()
            s_re[chunk], s_im[chunk] = deinterleave(
                held[:, chunk].reshape(2 * rows, LANES).astype(jnp.float32), chunk % 2
            )

        own, theirs = {}, {}
        pairs = 2
        for start in range(0, count, pairs):
            group = range(start, min(start + pairs, count))
            for chunk in group:
                gather(chunk)
            if start == 0:
                lend(me).wait_recv()
                sigma_two = prepare(1, lent[...].astype(jnp.float32))
            for chunk in group:
                theirs[chunk], = peaks((1, chunk))
                own[chunk], = peaks((0, chunk))
        lane = lax.broadcasted_iota(jnp.int32, (1, LANES), 1)

        def row(values, scale):
            out, most = jnp.zeros((1, LANES), jnp.float32), values[0]
            for chunk in range(count):
                out = jnp.where(lane == chunk, values[chunk] / scale, out)
                most = jnp.maximum(most, values[chunk])
            return out, jnp.broadcast_to(most / scale, (1, LANES))

        own_row, own_peak = row(own, sigma)
        their_row, their_peak = row(theirs, sigma_two)
        segment_row = jnp.maximum(own_row, their_row)
        mine[0] = their_row
        mine[1] = segment_row
        mine[2] = their_peak
        mine[3] = own_peak
        pl.semaphore_wait(ready, len(aside))
        across_copy(0, far_end).start()
        for seg in aside:
            side_copy(2, my_seg, end, seg).start()
        near_copy(end).start()
        across_copy(1, other).start()
        for seg in aside:
            side_copy(3, my_seg, me, seg).start()
        for chunk in range(count):
            block_copy(strain_ref.at[chunk], me, chunk, other, own_send).wait_send()
            block_copy(held.at[end, chunk], end, chunk, other, pass_send).wait_send()
        for seg in aside:
            side_copy(3, seg, me, my_seg).wait_recv()
        across_copy(1, me).wait_recv()
        template_peak = own_peak
        for seg in aside:
            template_peak = jnp.maximum(template_peak, side[seg])
        give_out(own_row, jnp.maximum(segment_row, across[...]), template_peak)
        across_copy(0, far_end).wait_send()
        across_copy(1, other).wait_send()
        near_copy(end).wait_send()
        for seg in aside:
            side_copy(2, my_seg, end, seg).wait_send()
            side_copy(3, my_seg, me, seg).wait_send()


def line(
    banks, segs, chunks,
    strain_hbm, tpl_hbm, bins_ref, first_hbm, last_hbm, odd_hbm, turn_hbm,
    out_ref,
    strain_ref, tpl_ref, held, tpl_re, tpl_im, work, first, last, odd, turn,
    row_bank, row_seg,
    input_sem, table_sem, right_sem, left_sem, recv_sem, bank_send, bank_recv, seg_send, seg_recv,
):
    me = lax.axis_index("bank")
    my_seg = lax.axis_index("seg")
    size = strain_ref.shape[0] // chunks
    rows = tpl_ref.shape[0] // 2

    def part(chunk):
        return pl.ds(chunk * size, size)

    def exists(device):
        return (device >= 0) & (device < banks)

    barrier = pltpu.get_barrier_semaphore()
    has_left, has_right = me > 0, me < banks - 1

    @pl.when(has_left)
    def _():
        pl.semaphore_signal(barrier, inc=1, device_id={"bank": me - 1}, device_id_type=MESH)

    @pl.when(has_right)
    def _():
        pl.semaphore_signal(barrier, inc=1, device_id={"bank": me + 1}, device_id_type=MESH)

    for step in range(1, segs):
        pl.semaphore_signal(
            barrier, inc=1, device_id={"seg": lax.rem(my_seg + step, segs)}, device_id_type=MESH
        )

    inputs = [
        pltpu.make_async_copy(source, target, input_sem.at[i])
        for i, (source, target) in enumerate(
            [(strain_hbm.at[part(chunk)], strain_ref.at[part(chunk)]) for chunk in range(chunks)]
            + [(tpl_hbm, tpl_ref)]
        )
    ]
    for load in inputs:
        load.start()
    loads = [
        pltpu.make_async_copy(source, target, table_sem.at[i])
        for i, (source, target) in enumerate(
            ((first_hbm, first), (odd_hbm, odd), (turn_hbm, turn), (last_hbm, last))
        )
    ]
    for load in loads:
        load.start()
    pl.semaphore_wait(barrier, has_left.astype(jnp.int32) + has_right.astype(jnp.int32) + segs - 1)

    def move(source, origin, chunk, step):
        sems = right_sem if step > 0 else left_sem
        return pltpu.make_async_remote_copy(
            src_ref=source,
            dst_ref=held.at[origin, part(chunk)],
            send_sem=sems.at[origin, chunk],
            recv_sem=recv_sem.at[origin, chunk],
            device_id={"bank": me + step},
            device_id_type=MESH,
        )

    for chunk in range(chunks):
        inputs[chunk].wait()
        for step in (1, -1):
            @pl.when(exists(me + step))
            def _():
                move(strain_ref.at[part(chunk)], me, chunk, step).start()

    held[me] = strain_ref[...]

    for load in inputs[chunks:] + loads:
        load.wait()
    position = lax.broadcasted_iota(jnp.int32, (2 * rows, LANES), 0) // 2 * LANES
    position = position + lax.broadcasted_iota(jnp.int32, (2 * rows, LANES), 1)
    keep = position < lax.shift_right_logical(jnp.full((1, 1), rows * LANES, jnp.int32), bins_ref[...])
    value = jnp.where(keep, tpl_ref[...].astype(jnp.float32), 0.0)
    work[...] = value
    tpl_re[...] = work[pl.ds(0, rows, stride=2), :]
    tpl_im[...] = work[pl.ds(1, rows, stride=2), :]
    sigma = jnp.sqrt(jnp.sum(value * value, keepdims=True) + EPSILON)

    def snr(seg):
        work[...] = held[:, seg].reshape(2 * rows, LANES).astype(jnp.float32)
        s_re = work[pl.ds(0, rows, stride=2), :]
        s_im = work[pl.ds(1, rows, stride=2), :]
        h_re, h_im = tpl_re[...], tpl_im[...]
        power, = transform([(h_re * s_re + h_im * s_im, h_re * s_im - h_im * s_re)], first, last, odd, turn)
        return jnp.sqrt(power) / sigma

    lane = lax.broadcasted_iota(jnp.int32, (8, LANES), 1)
    row_bank[me] = jnp.zeros((8, LANES), jnp.float32)

    for distance in range(1, banks):
        for chunk in range(chunks):
            for step in (1, -1):
                origin = me - step * distance

                @pl.when(exists(origin))
                def _():
                    block = held.at[origin, part(chunk)]
                    move(block, origin, chunk, step).wait_recv()

                    @pl.when(exists(me + step))
                    def _():
                        move(block, origin, chunk, step).start()

            if distance == banks - 1:
                for seg in range(chunk * size, (chunk + 1) * size):
                    row_bank[me] = jnp.where(lane == seg, snr(seg), row_bank[me])

    row_seg[my_seg] = row_bank[me]

    def tell(buffer, axis, index, peer, send, recv):
        return pltpu.make_async_remote_copy(
            src_ref=buffer.at[index],
            dst_ref=buffer.at[index],
            send_sem=send.at[peer],
            recv_sem=recv.at[index],
            device_id={axis: peer},
            device_id_type=MESH,
        )

    groups = (
        (row_bank, "bank", me, banks, bank_send, bank_recv),
        (row_seg, "seg", my_seg, segs, seg_send, seg_recv),
    )
    for buffer, axis, index, number, send, recv in groups:
        for step in range(1, number):
            tell(buffer, axis, index, lax.rem(index + step, number), send, recv).start()
    for chunk in range(chunks):
        for step in (1, -1):
            for distance in range(banks):
                origin = me - step * distance

                @pl.when(exists(origin) & exists(me + step))
                def _():
                    move(held.at[origin, part(chunk)], origin, chunk, step).wait_send()

    for buffer, axis, index, number, send, recv in reversed(groups):
        for step in range(1, number):
            other = lax.rem(index + step, number)
            tell(buffer, axis, other, other, send, recv).wait_recv()
    segment_peak = jnp.max(row_bank[...], axis=(0, 1))[None, :]
    template_peak = jnp.max(jnp.max(row_seg[...], axis=0)[:1], axis=1, keepdims=True)
    index = lax.broadcasted_iota(jnp.int32, (8, LANES), 0)
    out_ref[...] = jnp.where(index == 0, row_bank[me][:1], jnp.where(index == 1, segment_peak, template_peak))
    for buffer, axis, index, number, send, recv in groups:
        for step in range(1, number):
            tell(buffer, axis, index, lax.rem(index + step, number), send, recv).wait_send()


def unpack(out_ref, table_ref, segment_ref, template_ref):
    table_ref[...] = out_ref[0:1, : table_ref.shape[1]]
    segment_ref[...] = out_ref[1, : segment_ref.shape[0]]
    template_ref[...] = out_ref[2, :1]


def per_device(banks, segs, strain, templates, length_bins):
    count, _, width = strain.shape
    length = templates.shape[2]
    depth, rows = width // LANES, length // LANES
    first, last, odd, turn = tables(length)
    strain = strain.reshape(count, 2, depth, LANES).transpose(0, 2, 1, 3).reshape(count, 2 * depth, LANES)
    tpl = templates.reshape(2, rows, LANES).transpose(1, 0, 2).reshape(2 * rows, LANES)
    vmem = pl.BlockSpec(memory_space=pltpu.VMEM)
    hbm = pl.BlockSpec(memory_space=pltpu.HBM)
    dma = pltpu.SemaphoreType.DMA
    bf16, f32 = jnp.bfloat16, jnp.float32
    held = pltpu.VMEM((banks, count, 2 * depth, LANES), bf16)
    constants = [pltpu.VMEM(table.shape, table.dtype) for table in (first, last, odd, turn)]
    if banks == 4 and count > 2:
        body = functools.partial(middle, banks, segs)
        scratch = [
            pltpu.VMEM(strain.shape, bf16),
            pltpu.VMEM(tpl.shape, bf16),
            pltpu.VMEM(tpl.shape, bf16),
            pltpu.VMEM(tpl.shape, bf16),
            held,
            pltpu.VMEM((2, rows, LANES), f32),
            pltpu.VMEM((2, rows, LANES), f32),
            pltpu.VMEM((count, rows, LANES), f32),
            pltpu.VMEM((count, rows, LANES), f32),
            pltpu.VMEM((3, 2 * rows, LANES), f32),
            *constants,
            pltpu.VMEM((4, 1, LANES), f32),
            pltpu.VMEM((3, 1, LANES), f32),
            pltpu.VMEM((segs, 1, LANES), f32),
            pltpu.VMEM((1, LANES), f32),
            dma((count,)),
            dma((1,)),
            dma((4,)),
            dma((count,)),
            dma((count,)),
            dma((count,)),
            dma((banks, count)),
            dma((1,)),
            dma((1,)),
            dma((1,)),
            dma((1,)),
            dma((2, segs)),
            dma((segs,)),
            dma((2,)),
            dma((1,)),
            pltpu.SemaphoreType.REGULAR,
        ]
    else:
        chunks = count if banks <= 8 else 1
        body = functools.partial(line, banks, segs, chunks)
        scratch = [
            pltpu.VMEM(strain.shape, bf16),
            pltpu.VMEM(tpl.shape, bf16),
            held,
            pltpu.VMEM((rows, LANES), f32),
            pltpu.VMEM((rows, LANES), f32),
            pltpu.VMEM((2 * rows, LANES), f32),
            *constants,
            pltpu.VMEM((banks, 8, LANES), f32),
            pltpu.VMEM((segs, 8, LANES), f32),
            dma((chunks + 1,)),
            dma((4,)),
            dma((banks, chunks)),
            dma((banks, chunks)),
            dma((banks, chunks)),
            dma((banks,)),
            dma((banks,)),
            dma((segs,)),
            dma((segs,)),
        ]
    out = pl.pallas_call(
        body,
        out_shape=jax.ShapeDtypeStruct((8, LANES), f32),
        in_specs=[hbm, hbm, vmem, hbm, hbm, hbm, hbm],
        out_specs=vmem,
        scratch_shapes=scratch,
        compiler_params=pltpu.CompilerParams(collective_id=0, has_side_effects=True, vmem_limit_bytes=GRANT),
        name="search",
    )(strain, tpl, length_bins.reshape(1, 1), first, last, odd, turn)
    return pl.pallas_call(
        unpack,
        out_shape=[
            jax.ShapeDtypeStruct((1, count), f32),
            jax.ShapeDtypeStruct((count,), f32),
            jax.ShapeDtypeStruct((1,), f32),
        ],
        compiler_params=pltpu.CompilerParams(vmem_limit_bytes=1 << 20),
        in_specs=[vmem],
        out_specs=[vmem] * 3,
        name="unpack",
    )(out)


def solution(mesh):
    placed = (P(("grp", "seg"), None, "bank"), P("bank", None, None), P("bank"))
    return jax.shard_map(
        functools.partial(per_device, mesh.shape["bank"], mesh.shape["seg"]),
        mesh=mesh,
        in_specs=placed,
        out_specs=(P("bank", ("grp", "seg")), P(("grp", "seg")), P(("grp", "bank"))),
        check_vma=False,
    )
```

time: 22.4 us -> 20.3 us (0.906)
  Pallas kernels: 21 us -> 18.9 us
    pallas_call x2, Pallas kernels: 21 us -> 18.9 us  [the longest x1 18.3 us: per_device(): pl.pallas_call(body, out_shape=jax.ShapeDtypeStruct((8, LANES), f32), in_...]
where the time goes in v2:
time: 20.3 us; the launch traced here: 20.1 us
  Pallas kernels  18.9 us (93%)
  between operations  1.28 us (6%)
    pallas_call x1, Pallas kernels, per_device(): pl.pallas_call(body, out_shape=jax.ShapeDtypeStruct((8, LANES), f32), in_...  18.3 us
    pallas_call x1, Pallas kernels, per_device(): pl.pallas_call(unpack, out_shape=[jax.ShapeDtypeStruct((1, count), f32),...  0.52 us

profile of v2, /device:TPU:0, one launch (start us, length us, event | category | flops | bytes accessed | tf_op | source)
XLA Modules:
  0.0 20.1 jit_solution(9057714016535835168)
XLA Ops:
  1.3 18.3 %search.1.out_ref = f32[8,128]{1,0:T(8,128)S(1)} custom-call(bf16[4,128,128]{2,1,0:T(8,128)(2,1)} %bitcast.12, bf16[512,128]{1,0:T(8,128)(2,1)} %bitcast.13, s32[1,1]{1,0:T(1,128)} %bitcast.11.bins_ref, bf16[256,768]{1,0:T(8,128)(2,1)} %constant.8.clone.first_hbm, bf16[768,256]{1,0:T(8,128)(2,1)} %constant.9.clone.last_hbm, ...), custom_call_target="tpu_custom_call" | custom-call | tf_op jit(solution)/shard_map/search/pallas_call | solution.py:530
  19.6 0.5 %unpack.1 = (f32[1,4]{1,0:T(1,128)}, f32[4]{0:T(128)}, f32[1]{0:T(128)}) custom-call(f32[8,128]{1,0:T(8,128)S(1)} %search.1.out_ref), custom_call_target="tpu_custom_call" | custom-call | tf_op jit(solution)/shard_map/unpack/pallas_call | solution.py:539

commit v3 on v2

--- a/solution.py
+++ b/solution.py
@@ -12,6 +12,8 @@
 MESH = pl.DeviceIdType.MESH
 EPSILON = 1e-06
 LANES = 128
+WAYS = 4
+PARTS = 1
 GRANT = 56492032
 
 
@@ -23,21 +25,22 @@
 
 def tables(length):
     rows = length // LANES
-    half = rows // 2
+    depth = rows // WAYS
 
     def root(phase, period):
         angle = 2.0 * math.pi * (phase % period) / period
         return np.cos(angle), np.sin(angle)
 
-    r = np.arange(half)
+    r = np.arange(depth)
     c = np.arange(LANES)
-    row_c, row_s = root(np.outer(r, r), half)
+    row_c, row_s = root(np.outer(r, r), depth)
     first = np.block([[row_c, -row_s], [row_s, row_c]])
     col_c, col_s = root(np.outer(c, c), LANES)
     last = np.block([[col_c, col_s], [-col_s, col_c]])
-    odd = np.stack([np.broadcast_to(part[:, None], (half, LANES)) for part in root(r, rows)])
-    turn = [root(np.outer(2 * r + p, c), length) for p in (0, 1)]
-    turn = np.stack([np.concatenate([turn[0][i], turn[1][i]], axis=1) for i in (0, 1)])
+    twist = [root(r * way, rows) for way in range(1, WAYS)]
+    twist = np.stack([[np.broadcast_to(part[:, None], (depth, LANES)) for part in pair] for pair in twist])
+    turn = [root(np.outer(WAYS * r + way, c), length) for way in range(WAYS)]
+    turn = np.stack([np.concatenate([pair[i] for pair in turn], axis=1) for i in (0, 1)])
 
     def halves(matrix):
         high = matrix.astype(jnp.bfloat16)
@@ -48,59 +51,58 @@
     l_high, l_low = halves(last)
     first = np.concatenate([f_high, f_high, f_low], axis=1)
     last = np.concatenate([l_high, l_high, l_low], axis=0)
-    return first, last, odd.astype(np.float32), turn.astype(np.float32)
-
-
-def transform(products, first, last, odd, turn):
-    half = products[0][0].shape[0] // 2
-    many = len(products)
-    columns = []
-    for q_re, q_im in products:
-        even_re, even_im = q_re[:half] + q_re[half:], q_im[:half] + q_im[half:]
-        d_re, d_im = q_re[:half] - q_re[half:], q_im[:half] - q_im[half:]
-        odd_re = d_re * odd[0] - d_im * odd[1]
-        odd_im = d_re * odd[1] + d_im * odd[0]
-        columns.append(
-            jnp.concatenate(
-                [jnp.concatenate([even_re, odd_re], axis=1), jnp.concatenate([even_im, odd_im], axis=1)], axis=0
-            )
-        )
-    high, low = split(jnp.concatenate(columns, axis=1))
+    return first, last, twist.astype(np.float32), turn.astype(np.float32)
+
+
+def times(a, b):
+    return a[0] * b[0] - a[1] * b[1], a[0] * b[1] + a[1] * b[0]
+
+
+def transform(q_re, q_im, first, last, twist, turn):
+    depth = q_re.shape[0] // WAYS
+    (a, e), (b, f), (c, g), (d, h) = [
+        (q_re[depth * i : depth * (i + 1)], q_im[depth * i : depth * (i + 1)]) for i in range(WAYS)
+    ]
+    p_re, p_im, m_re, m_im = a + c, e + g, a - c, e - g
+    r_re, r_im, n_re, n_im = b + d, f + h, b - d, f - h
+    ways = [(p_re + r_re, p_im + r_im), (m_re - n_im, m_im + n_re), (p_re - r_re, p_im - r_im), (m_re + n_im, m_im - n_re)]
+    ways = ways[:1] + [times(ways[i], (twist[i - 1, 0], twist[i - 1, 1])) for i in range(1, WAYS)]
+    y = jnp.concatenate([jnp.concatenate([way[i] for way in ways], axis=1) for i in (0, 1)], axis=0)
+    high, low = split(y)
     u = jnp.dot(first[...], jnp.concatenate([high, low, high], axis=0), preferred_element_type=jnp.float32)
-    lines = []
-    for i in range(many):
-        part = u[:, 2 * LANES * i : 2 * LANES * (i + 1)]
-        u_re, u_im = part[:half], part[half:]
-        v_re = u_re * turn[0] - u_im * turn[1]
-        v_im = u_re * turn[1] + u_im * turn[0]
-        lines.append(jnp.concatenate([v_re[:, :LANES], v_im[:, :LANES]], axis=1))
-        lines.append(jnp.concatenate([v_re[:, LANES:], v_im[:, LANES:]], axis=1))
-    high, low = split(jnp.concatenate(lines, axis=0))
+    v_re, v_im = times((u[:depth], u[depth:]), (turn[0], turn[1]))
+    x = [
+        jnp.concatenate([v_re[:, LANES * i : LANES * (i + 1)], v_im[:, LANES * i : LANES * (i + 1)]], axis=1)
+        for i in range(WAYS)
+    ]
+    high, low = split(jnp.concatenate(x, axis=0))
     z = jnp.dot(jnp.concatenate([high, low, high], axis=1), last[...], preferred_element_type=jnp.float32)
     z_re, z_im = z[:, :LANES], z[:, LANES:]
-    power = z_re * z_re + z_im * z_im
-    return [jnp.max(power[2 * half * i : 2 * half * (i + 1)], keepdims=True) for i in range(many)]
+    return jnp.max(z_re * z_re + z_im * z_im, keepdims=True)
 
 
 def middle(
     banks, segs,
-    strain_hbm, tpl_hbm, bins_ref, first_hbm, last_hbm, odd_hbm, turn_hbm,
+    strain_hbm, tpl_hbm, bins_ref, first_hbm, last_hbm, twist_hbm, turn_hbm,
     out_ref,
-    strain_ref, tpl_ref, masked, lent, held, h_re, h_im, s_re, s_im, work, first, last, odd, turn,
+    strain_ref, tpl_ref, masked, lent, held, h_re, h_im, s_re, s_im, work, first, last, twist, turn,
     mine, near, side, across,
-    strain_sem, input_sem, table_sem, end_send, own_send, pass_send, block_recv, lend_send, lend_recv,
+    strain_sem, input_sem, table_sem, end_send, own_send, pass_send, block_recv, lend_send, lend_recv, share_send,
     near_send, near_recv, side_send, side_recv, across_send, across_recv, ready,
 ):
     me = lax.axis_index("bank")
     my_seg = lax.axis_index("seg")
     count = strain_ref.shape[0]
     rows = tpl_ref.shape[0] // 2
+    piece_rows = lent.shape[1]
     is_end = (me == 0) | (me == banks - 1)
     is_hub = jnp.logical_not(is_end)
     hub = jnp.where(me == 0, 1, banks - 2)
     other = banks - 1 - me
     end = jnp.where(me == 1, 0, banks - 1)
     far_end = banks - 1 - end
+    size = strain_ref.shape[1] // PARTS
+    parts = [pl.ds(i * size, size) for i in range(PARTS)]
     aside = [lax.rem(my_seg + step, segs) for step in range(1, segs)]
 
     barrier = pltpu.get_barrier_semaphore()
@@ -124,29 +126,47 @@
         for chunk in range(count)
     ]
     template = pltpu.make_async_copy(tpl_hbm, tpl_ref, input_sem.at[0])
+    own_piece = pl.ds(my_seg * piece_rows, piece_rows)
+    piece = pltpu.make_async_copy(tpl_hbm.at[own_piece], tpl_ref.at[own_piece], input_sem.at[1])
     loads = [
         pltpu.make_async_copy(source, target, table_sem.at[i])
-        for i, (source, target) in enumerate(((first_hbm, first), (odd_hbm, odd), (turn_hbm, turn), (last_hbm, last)))
+        for i, (source, target) in enumerate(((first_hbm, first), (twist_hbm, twist), (turn_hbm, turn), (last_hbm, last)))
     ]
-    for load in blocks + [template]:
+    @pl.when(is_end)
+    def _():
+        piece.start()
+
+    for load in blocks:
         load.start()
 
     @pl.when(is_hub)
     def _():
-        for load in loads:
+        for load in [template] + loads:
             load.start()
 
-    def block_copy(source, origin, chunk, to, send):
-        return pltpu.make_async_remote_copy(
-            src_ref=source, dst_ref=held.at[origin, chunk],
-            send_sem=send.at[chunk], recv_sem=block_recv.at[origin, chunk],
-            device_id={"bank": to}, device_id_type=MESH,
-        )
+    def block_copies(source, origin, chunk, to, send):
+        return [
+            pltpu.make_async_remote_copy(
+                src_ref=source.at[part], dst_ref=held.at[origin, chunk, part],
+                send_sem=send.at[chunk, i], recv_sem=block_recv.at[origin, chunk, i],
+                device_id={"bank": to}, device_id_type=MESH,
+            )
+            for i, part in enumerate(parts)
+        ]
+
+    def lender(chunk):
+        return {0: 0, count // 2: banks - 1}.get(chunk, -1)
 
     def lend(to):
         return pltpu.make_async_remote_copy(
-            src_ref=masked, dst_ref=lent, send_sem=lend_send.at[0], recv_sem=lend_recv.at[0],
+            src_ref=masked, dst_ref=lent.at[my_seg], send_sem=lend_send.at[0], recv_sem=lend_recv.at[my_seg],
             device_id={"bank": to}, device_id_type=MESH,
+        )
+
+    def share(index, to):
+        return pltpu.make_async_remote_copy(
+            src_ref=lent.at[index], dst_ref=lent.at[index], send_sem=share_send.at[to], recv_sem=lend_recv.at[index],
+            device_id={"seg": to}, device_id_type=MESH,
         )
 
     def near_copy(to):
@@ -168,9 +188,9 @@
             device_id={"bank": to}, device_id_type=MESH,
         )
 
-    def masked_template():
-        value = tpl_ref[...].astype(jnp.float32)
-        position = lax.broadcasted_iota(jnp.int32, value.shape, 0) // 2 * LANES
+    def mask(value, offset):
+        value = value.astype(jnp.float32)
+        position = (lax.broadcasted_iota(jnp.int32, value.shape, 0) + offset) // 2 * LANES
         position = position + lax.broadcasted_iota(jnp.int32, value.shape, 1)
         cutoff = lax.shift_right_logical(jnp.full((1, 1), rows * LANES, jnp.int32), bins_ref[...])
         return jnp.where(position < cutoff, value, 0.0)
@@ -181,15 +201,20 @@
 
     @pl.when(is_end)
     def _():
-        template.wait()
-        masked[...] = masked_template().astype(jnp.bfloat16)
+        piece.wait()
+        masked[...] = mask(tpl_ref[own_piece, :], my_seg * piece_rows).astype(jnp.bfloat16)
         pl.semaphore_wait(barrier, 1)
         for chunk in range(count):
+            @pl.when(me == lender(chunk))
+            def _():
+                lend(hub).start()
+
             blocks[chunk].wait()
-            block_copy(strain_ref.at[chunk], me, chunk, hub, end_send).start()
-        lend(hub).start()
+            for copy in block_copies(strain_ref.at[chunk], me, chunk, hub, end_send):
+                copy.start()
         for chunk in range(count):
-            block_copy(strain_ref.at[chunk], me, chunk, hub, end_send).wait_send()
+            for copy in block_copies(strain_ref.at[chunk], me, chunk, hub, end_send):
+                copy.wait_send()
         lend(hub).wait_send()
         for seg in aside:
             side_copy(2, seg, me, my_seg).wait_recv()
@@ -212,47 +237,51 @@
         a, b, c, d = s_re[seg], s_im[seg], h_re[slot], h_im[slot]
         return c * a + d * b, c * b - d * a
 
-    def peaks(*pairs):
-        return [jnp.sqrt(power) for power in transform([product(*pair) for pair in pairs], first, last, odd, turn)]
+    def peak(slot, seg):
+        return jnp.sqrt(transform(*product(slot, seg), first, last, twist, turn))
 
     @pl.when(is_hub)
     def _():
         pl.semaphore_wait(barrier, 2 + len(aside))
         for chunk in range(count):
             blocks[chunk].wait()
-            block_copy(strain_ref.at[chunk], me, chunk, other, own_send).start()
+            for copy in block_copies(strain_ref.at[chunk], me, chunk, other, own_send):
+                copy.start()
         for seg in aside:
             signal(ready, {"seg": seg})
         template.wait()
-        sigma = prepare(0, masked_template())
-        for chunk in range(count):
-            held[me, chunk] = strain_ref[chunk]
+        sigma = prepare(0, mask(tpl_ref[...], 0))
         for load in loads:
             load.wait()
         for chunk in range(count):
+            held[me, chunk] = strain_ref[chunk]
+        for chunk in range(count):
+            @pl.when(end == lender(chunk))
+            def _():
+                lend(me).wait_recv()
+                for seg in aside:
+                    share(my_seg, seg).start()
+
             block = held.at[end, chunk]
-            block_copy(block, end, chunk, me, pass_send).wait_recv()
-            block_copy(block, end, chunk, other, pass_send).start()
-
-        def gather(chunk):
-            for origin in (other, far_end):
-                block_copy(held.at[origin, chunk], origin, chunk, me, pass_send).wait_recv()
-            s_re[chunk], s_im[chunk] = deinterleave(
-                held[:, chunk].reshape(2 * rows, LANES).astype(jnp.float32), chunk % 2
-            )
-
-        own, theirs = {}, {}
-        pairs = 2
-        for start in range(0, count, pairs):
-            group = range(start, min(start + pairs, count))
-            for chunk in group:
-                gather(chunk)
-            if start == 0:
-                lend(me).wait_recv()
-                sigma_two = prepare(1, lent[...].astype(jnp.float32))
-            for chunk in group:
-                theirs[chunk], = peaks((1, chunk))
-                own[chunk], = peaks((0, chunk))
+            arriving = block_copies(block, end, chunk, me, pass_send)
+            for copy, onward in zip(arriving, block_copies(block, end, chunk, other, pass_send)):
+                copy.wait_recv()
+                onward.start()
+
+        def gather(*chunks):
+            for chunk in chunks:
+                for origin in (other, far_end):
+                    for copy in block_copies(held.at[origin, chunk], origin, chunk, me, pass_send):
+                        copy.wait_recv()
+                s_re[chunk], s_im[chunk] = deinterleave(
+                    held[:, chunk].reshape(2 * rows, LANES).astype(jnp.float32), chunk % 2
+                )
+
+        def borrow():
+            for seg in aside:
+                share(seg, my_seg).wait_recv()
+            return prepare(1, lent[...].reshape(2 * rows, LANES).astype(jnp.float32))
+
         lane = lax.broadcasted_iota(jnp.int32, (1, LANES), 1)
 
         def row(values, scale):
@@ -262,31 +291,71 @@
                 most = jnp.maximum(most, values[chunk])
             return out, jnp.broadcast_to(most / scale, (1, LANES))
 
-        own_row, own_peak = row(own, sigma)
-        their_row, their_peak = row(theirs, sigma_two)
-        segment_row = jnp.maximum(own_row, their_row)
-        mine[0] = their_row
-        mine[1] = segment_row
-        mine[2] = their_peak
-        mine[3] = own_peak
-        pl.semaphore_wait(ready, len(aside))
-        across_copy(0, far_end).start()
-        for seg in aside:
-            side_copy(2, my_seg, end, seg).start()
-        near_copy(end).start()
-        across_copy(1, other).start()
-        for seg in aside:
-            side_copy(3, my_seg, me, seg).start()
+        def send_side(sigma_two):
+            mine[0], mine[2] = row(theirs, sigma_two)
+            pl.semaphore_wait(ready, len(aside))
+            for seg in aside:
+                side_copy(2, my_seg, end, seg).start()
+
+        def send_rest():
+            mine[4], mine[3] = row(own, sigma)
+            mine[1] = jnp.maximum(mine[0], mine[4])
+            across_copy(0, far_end).start()
+            near_copy(end).start()
+            across_copy(1, other).start()
+            for seg in aside:
+                side_copy(3, my_seg, me, seg).start()
+
+        early, late = range(count // 2), range(count // 2, count)
+        own, theirs = {}, {}
+
+        @pl.when(me == 1)
+        def _():
+            sigma_two = borrow()
+            gather(0)
+            theirs[0] = peak(1, 0)
+            own[0] = peak(0, 0)
+            gather(1)
+            theirs[1] = peak(1, 1)
+            own[1] = peak(0, 1)
+            gather(2, 3)
+            theirs[2] = peak(1, 2)
+            theirs[3] = peak(1, 3)
+            send_side(sigma_two)
+            own[2] = peak(0, 2)
+            own[3] = peak(0, 3)
+            send_rest()
+
+        @pl.when(me != 1)
+        def _():
+            gather(0, 1)
+            own[0] = peak(0, 0)
+            own[1] = peak(0, 1)
+            gather(2, 3)
+            own[2] = peak(0, 2)
+            own[3] = peak(0, 3)
+            sigma_two = borrow()
+            theirs[0] = peak(1, 0)
+            theirs[1] = peak(1, 1)
+            theirs[2] = peak(1, 2)
+            theirs[3] = peak(1, 3)
+            send_side(sigma_two)
+            send_rest()
+
+        for seg in aside:
+            share(my_seg, seg).wait_send()
         for chunk in range(count):
-            block_copy(strain_ref.at[chunk], me, chunk, other, own_send).wait_send()
-            block_copy(held.at[end, chunk], end, chunk, other, pass_send).wait_send()
+            for copy in block_copies(strain_ref.at[chunk], me, chunk, other, own_send):
+                copy.wait_send()
+            for copy in block_copies(held.at[end, chunk], end, chunk, other, pass_send):
+                copy.wait_send()
         for seg in aside:
             side_copy(3, seg, me, my_seg).wait_recv()
         across_copy(1, me).wait_recv()
-        template_peak = own_peak
+        template_peak = mine[3]
         for seg in aside:
             template_peak = jnp.maximum(template_peak, side[seg])
-        give_out(own_row, jnp.maximum(segment_row, across[...]), template_peak)
+        give_out(mine[4], jnp.maximum(mine[1], across[...]), template_peak)
         across_copy(0, far_end).wait_send()
         across_copy(1, other).wait_send()
         near_copy(end).wait_send()
@@ -297,9 +366,9 @@
 
 def line(
     banks, segs, chunks,
-    strain_hbm, tpl_hbm, bins_ref, first_hbm, last_hbm, odd_hbm, turn_hbm,
+    strain_hbm, tpl_hbm, bins_ref, first_hbm, last_hbm, twist_hbm, turn_hbm,
     out_ref,
-    strain_ref, tpl_ref, held, tpl_re, tpl_im, work, first, last, odd, turn,
+    strain_ref, tpl_ref, held, tpl_re, tpl_im, work, first, last, twist, turn,
     row_bank, row_seg,
     input_sem, table_sem, right_sem, left_sem, recv_sem, bank_send, bank_recv, seg_send, seg_recv,
 ):
@@ -342,7 +411,7 @@
     loads = [
         pltpu.make_async_copy(source, target, table_sem.at[i])
         for i, (source, target) in enumerate(
-            ((first_hbm, first), (odd_hbm, odd), (turn_hbm, turn), (last_hbm, last))
+            ((first_hbm, first), (twist_hbm, twist), (turn_hbm, turn), (last_hbm, last))
         )
     ]
     for load in loads:
@@ -385,8 +454,8 @@
         s_re = work[pl.ds(0, rows, stride=2), :]
         s_im = work[pl.ds(1, rows, stride=2), :]
         h_re, h_im = tpl_re[...], tpl_im[...]
-        power, = transform([(h_re * s_re + h_im * s_im, h_re * s_im - h_im * s_re)], first, last, odd, turn)
-        return jnp.sqrt(power) / sigma
+        q_re, q_im = h_re * s_re + h_im * s_im, h_re * s_im - h_im * s_re
+        return jnp.sqrt(transform(q_re, q_im, first, last, twist, turn)) / sigma
 
     lane = lax.broadcasted_iota(jnp.int32, (8, LANES), 1)
     row_bank[me] = jnp.zeros((8, LANES), jnp.float32)
@@ -460,7 +529,7 @@
     count, _, width = strain.shape
     length = templates.shape[2]
     depth, rows = width // LANES, length // LANES
-    first, last, odd, turn = tables(length)
+    first, last, twist, turn = tables(length)
     strain = strain.reshape(count, 2, depth, LANES).transpose(0, 2, 1, 3).reshape(count, 2 * depth, LANES)
     tpl = templates.reshape(2, rows, LANES).transpose(1, 0, 2).reshape(2 * rows, LANES)
     vmem = pl.BlockSpec(memory_space=pltpu.VMEM)
@@ -468,14 +537,15 @@
     dma = pltpu.SemaphoreType.DMA
     bf16, f32 = jnp.bfloat16, jnp.float32
     held = pltpu.VMEM((banks, count, 2 * depth, LANES), bf16)
-    constants = [pltpu.VMEM(table.shape, table.dtype) for table in (first, last, odd, turn)]
+    constants = [pltpu.VMEM(table.shape, table.dtype) for table in (first, last, twist, turn)]
     if banks == 4 and count > 2:
         body = functools.partial(middle, banks, segs)
+        piece_rows = 2 * rows // segs
         scratch = [
             pltpu.VMEM(strain.shape, bf16),
             pltpu.VMEM(tpl.shape, bf16),
-            pltpu.VMEM(tpl.shape, bf16),
-            pltpu.VMEM(tpl.shape, bf16),
+            pltpu.VMEM((piece_rows, LANES), bf16),
+            pltpu.VMEM((segs, piece_rows, LANES), bf16),
             held,
             pltpu.VMEM((2, rows, LANES), f32),
             pltpu.VMEM((2, rows, LANES), f32),
@@ -483,19 +553,20 @@
             pltpu.VMEM((count, rows, LANES), f32),
             pltpu.VMEM((3, 2 * rows, LANES), f32),
             *constants,
-            pltpu.VMEM((4, 1, LANES), f32),
+            pltpu.VMEM((5, 1, LANES), f32),
             pltpu.VMEM((3, 1, LANES), f32),
             pltpu.VMEM((segs, 1, LANES), f32),
             pltpu.VMEM((1, LANES), f32),
             dma((count,)),
+            dma((2,)),
+            dma((4,)),
+            dma((count, PARTS)),
+            dma((count, PARTS)),
+            dma((count, PARTS)),
+            dma((banks, count, PARTS)),
             dma((1,)),
-            dma((4,)),
-            dma((count,)),
-            dma((count,)),
-            dma((count,)),
-            dma((banks, count)),
-            dma((1,)),
-            dma((1,)),
+            dma((segs,)),
+            dma((segs,)),
             dma((1,)),
             dma((1,)),
             dma((2, segs)),
@@ -535,7 +606,7 @@
         scratch_shapes=scratch,
         compiler_params=pltpu.CompilerParams(collective_id=0, has_side_effects=True, vmem_limit_bytes=GRANT),
         name="search",
-    )(strain, tpl, length_bins.reshape(1, 1), first, last, odd, turn)
+    )(strain, tpl, length_bins.reshape(1, 1), first, last, twist, turn)
     return pl.pallas_call(
         unpack,
         out_shape=[

time: 20.3 us -> 19.4 us (0.956)
  Pallas kernels: 18.9 us -> 17.9 us
    pallas_call x1, Pallas kernels: 18.3 us -> 17.4 us  [per_device(): pl.pallas_call(body, out_shape=jax.ShapeDtypeStruct((8, LANES), f32), in_...]
where the time goes in v3:
time: 19.4 us; the launch traced here: 19.2 us
  Pallas kernels  17.9 us (92%)
  between operations  1.28 us (7%)
    pallas_call x1, Pallas kernels, per_device(): pl.pallas_call(body, out_shape=jax.ShapeDtypeStruct((8, LANES), f32), in_...  17.4 us
    pallas_call x1, Pallas kernels, per_device(): pl.pallas_call(unpack, out_shape=[jax.ShapeDtypeStruct((1, count), f32),...  0.52 us

profile of v3, /device:TPU:0, one launch (start us, length us, event | category | flops | bytes accessed | tf_op | source)
XLA Modules:
  0.0 19.2 jit_solution(83270299849690465)
XLA Ops:
  1.3 17.4 %search.1.out_ref = f32[8,128]{1,0:T(8,128)S(1)} custom-call(bf16[4,128,128]{2,1,0:T(8,128)(2,1)} %bitcast.12, bf16[512,128]{1,0:T(8,128)(2,1)} %bitcast.13, s32[1,1]{1,0:T(1,128)} %bitcast.11.bins_ref, bf16[128,384]{1,0:T(8,128)(2,1)} %constant.8.clone.first_hbm, bf16[768,256]{1,0:T(8,128)(2,1)} %constant.9.clone.last_hbm, ...), custom_call_target="tpu_custom_call" | custom-call | tf_op jit(solution)/shard_map/search/pallas_call | solution.py:601
  18.7 0.5 %unpack.1 = (f32[1,4]{1,0:T(1,128)}, f32[4]{0:T(128)}, f32[1]{0:T(128)}) custom-call(f32[8,128]{1,0:T(8,128)S(1)} %search.1.out_ref), custom_call_target="tpu_custom_call" | custom-call | tf_op jit(solution)/shard_map/unpack/pallas_call | solution.py:610

commit v4 on v3

--- a/solution.py
+++ b/solution.py
@@ -13,7 +13,6 @@
 EPSILON = 1e-06
 LANES = 128
 WAYS = 4
-PARTS = 1
 GRANT = 56492032
 
 
@@ -37,10 +36,9 @@
     first = np.block([[row_c, -row_s], [row_s, row_c]])
     col_c, col_s = root(np.outer(c, c), LANES)
     last = np.block([[col_c, col_s], [-col_s, col_c]])
-    twist = [root(r * way, rows) for way in range(1, WAYS)]
-    twist = np.stack([[np.broadcast_to(part[:, None], (depth, LANES)) for part in pair] for pair in twist])
+    twist = [root(np.outer(r * way, np.ones(LANES, int)), rows) for way in range(1, WAYS)]
     turn = [root(np.outer(WAYS * r + way, c), length) for way in range(WAYS)]
-    turn = np.stack([np.concatenate([pair[i] for pair in turn], axis=1) for i in (0, 1)])
+    spin = np.stack([np.stack(pair) for pair in turn + twist])
 
     def halves(matrix):
         high = matrix.astype(jnp.bfloat16)
@@ -51,14 +49,14 @@
     l_high, l_low = halves(last)
     first = np.concatenate([f_high, f_high, f_low], axis=1)
     last = np.concatenate([l_high, l_high, l_low], axis=0)
-    return first, last, twist.astype(np.float32), turn.astype(np.float32)
+    return first, last, spin.astype(np.float32)
 
 
 def times(a, b):
     return a[0] * b[0] - a[1] * b[1], a[0] * b[1] + a[1] * b[0]
 
 
-def transform(q_re, q_im, first, last, twist, turn):
+def transform(q_re, q_im, first, last, spin):
     depth = q_re.shape[0] // WAYS
     (a, e), (b, f), (c, g), (d, h) = [
         (q_re[depth * i : depth * (i + 1)], q_im[depth * i : depth * (i + 1)]) for i in range(WAYS)
@@ -66,15 +64,14 @@
     p_re, p_im, m_re, m_im = a + c, e + g, a - c, e - g
     r_re, r_im, n_re, n_im = b + d, f + h, b - d, f - h
     ways = [(p_re + r_re, p_im + r_im), (m_re - n_im, m_im + n_re), (p_re - r_re, p_im - r_im), (m_re + n_im, m_im - n_re)]
-    ways = ways[:1] + [times(ways[i], (twist[i - 1, 0], twist[i - 1, 1])) for i in range(1, WAYS)]
+    ways = ways[:1] + [times(ways[i], (spin[WAYS + i - 1, 0], spin[WAYS + i - 1, 1])) for i in range(1, WAYS)]
     y = jnp.concatenate([jnp.concatenate([way[i] for way in ways], axis=1) for i in (0, 1)], axis=0)
     high, low = split(y)
     u = jnp.dot(first[...], jnp.concatenate([high, low, high], axis=0), preferred_element_type=jnp.float32)
-    v_re, v_im = times((u[:depth], u[depth:]), (turn[0], turn[1]))
-    x = [
-        jnp.concatenate([v_re[:, LANES * i : LANES * (i + 1)], v_im[:, LANES * i : LANES * (i + 1)]], axis=1)
-        for i in range(WAYS)
-    ]
+    x = []
+    for i in range(WAYS):
+        part = u[:, LANES * i : LANES * (i + 1)]
+        x.append(jnp.concatenate(times((part[:depth], part[depth:]), (spin[i, 0], spin[i, 1])), axis=1))
     high, low = split(jnp.concatenate(x, axis=0))
     z = jnp.dot(jnp.concatenate([high, low, high], axis=1), last[...], preferred_element_type=jnp.float32)
     z_re, z_im = z[:, :LANES], z[:, LANES:]
@@ -83,12 +80,12 @@
 
 def middle(
     banks, segs,
-    strain_hbm, tpl_hbm, bins_ref, first_hbm, last_hbm, twist_hbm, turn_hbm,
+    strain_hbm, tpl_hbm, bins_ref, first_hbm, last_hbm, spin_hbm,
     out_ref,
-    strain_ref, tpl_ref, masked, lent, held, h_re, h_im, s_re, s_im, work, first, last, twist, turn,
-    mine, near, side, across,
-    strain_sem, input_sem, table_sem, end_send, own_send, pass_send, block_recv, lend_send, lend_recv, share_send,
-    near_send, near_recv, side_send, side_recv, across_send, across_recv, ready,
+    strain_ref, tpl_ref, masked, lent, held, h_re, h_im, s_re, s_im, work, first, last, spin,
+    mine, inbox,
+    strain_sem, tpl_sem, table_sem, block_send, pass_send, end_recv, other_recv, far_recv,
+    lend_send, lend_recv, share_send, share_recv, row_send, row_recv, ready,
 ):
     me = lax.axis_index("bank")
     my_seg = lax.axis_index("seg")
@@ -101,8 +98,7 @@
     other = banks - 1 - me
     end = jnp.where(me == 1, 0, banks - 1)
     far_end = banks - 1 - end
-    size = strain_ref.shape[1] // PARTS
-    parts = [pl.ds(i * size, size) for i in range(PARTS)]
+    early, late = range(count // 2), range(count // 2, count)
     aside = [lax.rem(my_seg + step, segs) for step in range(1, segs)]
 
     barrier = pltpu.get_barrier_semaphore()
@@ -121,72 +117,62 @@
         for seg in aside:
             signal(barrier, {"seg": seg})
 
-    blocks = [
-        pltpu.make_async_copy(strain_hbm.at[chunk], strain_ref.at[chunk], strain_sem.at[chunk])
-        for chunk in range(count)
-    ]
-    template = pltpu.make_async_copy(tpl_hbm, tpl_ref, input_sem.at[0])
     own_piece = pl.ds(my_seg * piece_rows, piece_rows)
-    piece = pltpu.make_async_copy(tpl_hbm.at[own_piece], tpl_ref.at[own_piece], input_sem.at[1])
+    piece = pltpu.make_async_copy(tpl_hbm.at[own_piece], tpl_ref.at[own_piece], tpl_sem)
+    template = pltpu.make_async_copy(tpl_hbm, tpl_ref, tpl_sem)
+    blocks = pltpu.make_async_copy(strain_hbm, strain_ref, strain_sem)
     loads = [
         pltpu.make_async_copy(source, target, table_sem.at[i])
-        for i, (source, target) in enumerate(((first_hbm, first), (twist_hbm, twist), (turn_hbm, turn), (last_hbm, last)))
+        for i, (source, target) in enumerate(((first_hbm, first), (spin_hbm, spin), (last_hbm, last)))
     ]
+
     @pl.when(is_end)
     def _():
         piece.start()
 
-    for load in blocks:
-        load.start()
+    blocks.start()
 
     @pl.when(is_hub)
     def _():
         for load in [template] + loads:
             load.start()
 
-    def block_copies(source, origin, chunk, to, send):
-        return [
-            pltpu.make_async_remote_copy(
-                src_ref=source.at[part], dst_ref=held.at[origin, chunk, part],
-                send_sem=send.at[chunk, i], recv_sem=block_recv.at[origin, chunk, i],
-                device_id={"bank": to}, device_id_type=MESH,
-            )
-            for i, part in enumerate(parts)
-        ]
+    def remote(source, target, sent, arrived, place):
+        return pltpu.make_async_remote_copy(
+            src_ref=source, dst_ref=target, send_sem=sent, recv_sem=arrived, device_id=place, device_id_type=MESH
+        )
+
+    def from_end(origin, chunk, to):
+        return remote(strain_ref.at[chunk], held.at[origin, chunk], block_send, end_recv.at[chunk], {"bank": to})
+
+    def from_hub(origin, chunk, to):
+        return remote(strain_ref.at[chunk], held.at[origin, chunk], block_send, other_recv, {"bank": to})
+
+    def passed(origin, chunk, to):
+        block = held.at[origin, chunk]
+        return remote(block, block, pass_send, far_recv.at[min(chunk, late[0])], {"bank": to})
+
+    def all_of(block, sent, arrived):
+        return remote(block, block, sent, arrived, {"bank": hub})
 
     def lender(chunk):
-        return {0: 0, count // 2: banks - 1}.get(chunk, -1)
+        return {0: 0, late[0]: banks - 1}.get(chunk, -1)
 
     def lend(to):
-        return pltpu.make_async_remote_copy(
-            src_ref=masked, dst_ref=lent.at[my_seg], send_sem=lend_send.at[0], recv_sem=lend_recv.at[my_seg],
-            device_id={"bank": to}, device_id_type=MESH,
-        )
-
-    def share(index, to):
-        return pltpu.make_async_remote_copy(
-            src_ref=lent.at[index], dst_ref=lent.at[index], send_sem=share_send.at[to], recv_sem=lend_recv.at[index],
-            device_id={"seg": to}, device_id_type=MESH,
-        )
-
-    def near_copy(to):
-        return pltpu.make_async_remote_copy(
-            src_ref=mine.at[pl.ds(0, 3)], dst_ref=near, send_sem=near_send.at[0], recv_sem=near_recv.at[0],
-            device_id={"bank": to}, device_id_type=MESH,
-        )
-
-    def side_copy(row, origin, bank, to):
-        return pltpu.make_async_remote_copy(
-            src_ref=mine.at[row], dst_ref=side.at[origin],
-            send_sem=side_send.at[row // 3, to], recv_sem=side_recv.at[origin],
-            device_id={"bank": bank, "seg": to}, device_id_type=MESH,
-        )
-
-    def across_copy(which, to):
-        return pltpu.make_async_remote_copy(
-            src_ref=mine.at[1], dst_ref=across, send_sem=across_send.at[which], recv_sem=across_recv.at[0],
-            device_id={"bank": to}, device_id_type=MESH,
-        )
+        return remote(masked, lent.at[my_seg], lend_send, lend_recv, {"bank": to})
+
+    def share(to):
+        return remote(lent.at[my_seg], lent.at[my_seg], share_send, share_recv, {"seg": to})
+
+    others = lent.at[pl.ds(0, segs - 1)]
+    near, across, side = 0, 3, 4
+
+    def row_copy(row, target, place, number=1):
+        part = pl.ds(row, number)
+        return remote(mine.at[part], inbox.at[pl.ds(target, number)], row_send, row_recv, place)
+
+    def rows_of(number):
+        return all_of(inbox.at[pl.ds(0, number)], row_send, row_recv)
 
     def mask(value, offset):
         value = value.astype(jnp.float32)
@@ -196,7 +182,10 @@
         return jnp.where(position < cutoff, value, 0.0)
 
     def give_out(table, segment_peak, template_peak):
+        for seg in aside:
+            template_peak = jnp.maximum(template_peak, inbox[side + seg])
         line = lax.broadcasted_iota(jnp.int32, (8, LANES), 0)
+        segment_peak = jnp.maximum(segment_peak, inbox[across])
         out_ref[...] = jnp.where(line == 0, table, jnp.where(line == 1, segment_peak, template_peak))
 
     @pl.when(is_end)
@@ -204,26 +193,17 @@
         piece.wait()
         masked[...] = mask(tpl_ref[own_piece, :], my_seg * piece_rows).astype(jnp.bfloat16)
         pl.semaphore_wait(barrier, 1)
+        blocks.wait()
         for chunk in range(count):
             @pl.when(me == lender(chunk))
             def _():
                 lend(hub).start()
 
-            blocks[chunk].wait()
-            for copy in block_copies(strain_ref.at[chunk], me, chunk, hub, end_send):
-                copy.start()
-        for chunk in range(count):
-            for copy in block_copies(strain_ref.at[chunk], me, chunk, hub, end_send):
-                copy.wait_send()
+            from_end(me, chunk, hub).start()
+        all_of(strain_ref, block_send, other_recv).wait_send()
         lend(hub).wait_send()
-        for seg in aside:
-            side_copy(2, seg, me, my_seg).wait_recv()
-        near_copy(me).wait_recv()
-        across_copy(0, me).wait_recv()
-        template_peak = near[2]
-        for seg in aside:
-            template_peak = jnp.maximum(template_peak, side[seg])
-        give_out(near[0], jnp.maximum(near[1], across[...]), template_peak)
+        rows_of(4 + len(aside)).wait_recv()
+        give_out(inbox[near], inbox[near + 1], inbox[near + 2])
 
     def deinterleave(value, slot):
         work[slot] = value
@@ -233,53 +213,46 @@
         h_re[slot], h_im[slot] = deinterleave(value, 2)
         return jnp.sqrt(jnp.sum(value * value, keepdims=True) + EPSILON)
 
-    def product(slot, seg):
+    def peak(slot, seg):
         a, b, c, d = s_re[seg], s_im[seg], h_re[slot], h_im[slot]
-        return c * a + d * b, c * b - d * a
-
-    def peak(slot, seg):
-        return jnp.sqrt(transform(*product(slot, seg), first, last, twist, turn))
+        return jnp.sqrt(transform(c * a + d * b, c * b - d * a, first, last, spin))
 
     @pl.when(is_hub)
     def _():
         pl.semaphore_wait(barrier, 2 + len(aside))
+        blocks.wait()
         for chunk in range(count):
-            blocks[chunk].wait()
-            for copy in block_copies(strain_ref.at[chunk], me, chunk, other, own_send):
-                copy.start()
+            from_hub(me, chunk, other).start()
         for seg in aside:
             signal(ready, {"seg": seg})
         template.wait()
         sigma = prepare(0, mask(tpl_ref[...], 0))
         for load in loads:
             load.wait()
-        for chunk in range(count):
-            held[me, chunk] = strain_ref[chunk]
+        held[me] = strain_ref[...]
         for chunk in range(count):
             @pl.when(end == lender(chunk))
             def _():
                 lend(me).wait_recv()
                 for seg in aside:
-                    share(my_seg, seg).start()
-
-            block = held.at[end, chunk]
-            arriving = block_copies(block, end, chunk, me, pass_send)
-            for copy, onward in zip(arriving, block_copies(block, end, chunk, other, pass_send)):
-                copy.wait_recv()
-                onward.start()
+                    share(seg).start()
+
+            from_end(end, chunk, me).wait_recv()
+            passed(end, chunk, other).start()
+        all_of(held.at[other], block_send, other_recv).wait_recv()
 
         def gather(*chunks):
+            if len(chunks) > 1:
+                all_of(held.at[far_end, pl.ds(chunks[0], len(chunks))], pass_send, far_recv.at[chunks[0]]).wait_recv()
+            else:
+                passed(far_end, chunks[0], me).wait_recv()
             for chunk in chunks:
-                for origin in (other, far_end):
-                    for copy in block_copies(held.at[origin, chunk], origin, chunk, me, pass_send):
-                        copy.wait_recv()
                 s_re[chunk], s_im[chunk] = deinterleave(
                     held[:, chunk].reshape(2 * rows, LANES).astype(jnp.float32), chunk % 2
                 )
 
         def borrow():
-            for seg in aside:
-                share(seg, my_seg).wait_recv()
+            all_of(others, share_send, share_recv).wait_recv()
             return prepare(1, lent[...].reshape(2 * rows, LANES).astype(jnp.float32))
 
         lane = lax.broadcasted_iota(jnp.int32, (1, LANES), 1)
@@ -295,80 +268,62 @@
             mine[0], mine[2] = row(theirs, sigma_two)
             pl.semaphore_wait(ready, len(aside))
             for seg in aside:
-                side_copy(2, my_seg, end, seg).start()
+                row_copy(2, side + my_seg, {"bank": end, "seg": seg}).start()
 
         def send_rest():
             mine[4], mine[3] = row(own, sigma)
             mine[1] = jnp.maximum(mine[0], mine[4])
-            across_copy(0, far_end).start()
-            near_copy(end).start()
-            across_copy(1, other).start()
+            row_copy(1, across, {"bank": far_end}).start()
+            row_copy(0, near, {"bank": end}, 3).start()
+            row_copy(1, across, {"bank": other}).start()
             for seg in aside:
-                side_copy(3, my_seg, me, seg).start()
-
-        early, late = range(count // 2), range(count // 2, count)
+                row_copy(3, side + my_seg, {"seg": seg}).start()
+
         own, theirs = {}, {}
 
         @pl.when(me == 1)
         def _():
             sigma_two = borrow()
-            gather(0)
-            theirs[0] = peak(1, 0)
-            own[0] = peak(0, 0)
-            gather(1)
-            theirs[1] = peak(1, 1)
-            own[1] = peak(0, 1)
-            gather(2, 3)
-            theirs[2] = peak(1, 2)
-            theirs[3] = peak(1, 3)
+            for chunk in early:
+                gather(chunk)
+                theirs[chunk] = peak(1, chunk)
+                own[chunk] = peak(0, chunk)
+            gather(*late)
+            for chunk in late:
+                theirs[chunk] = peak(1, chunk)
             send_side(sigma_two)
-            own[2] = peak(0, 2)
-            own[3] = peak(0, 3)
+            for chunk in late:
+                own[chunk] = peak(0, chunk)
             send_rest()
 
         @pl.when(me != 1)
         def _():
-            gather(0, 1)
-            own[0] = peak(0, 0)
-            own[1] = peak(0, 1)
-            gather(2, 3)
-            own[2] = peak(0, 2)
-            own[3] = peak(0, 3)
+            for chunk in early:
+                gather(chunk)
+            for chunk in early:
+                own[chunk] = peak(0, chunk)
+            gather(*late)
+            for chunk in late:
+                own[chunk] = peak(0, chunk)
             sigma_two = borrow()
-            theirs[0] = peak(1, 0)
-            theirs[1] = peak(1, 1)
-            theirs[2] = peak(1, 2)
-            theirs[3] = peak(1, 3)
+            for chunk in range(count):
+                theirs[chunk] = peak(1, chunk)
             send_side(sigma_two)
             send_rest()
 
-        for seg in aside:
-            share(my_seg, seg).wait_send()
-        for chunk in range(count):
-            for copy in block_copies(strain_ref.at[chunk], me, chunk, other, own_send):
-                copy.wait_send()
-            for copy in block_copies(held.at[end, chunk], end, chunk, other, pass_send):
-                copy.wait_send()
-        for seg in aside:
-            side_copy(3, seg, me, my_seg).wait_recv()
-        across_copy(1, me).wait_recv()
-        template_peak = mine[3]
-        for seg in aside:
-            template_peak = jnp.maximum(template_peak, side[seg])
-        give_out(mine[4], jnp.maximum(mine[1], across[...]), template_peak)
-        across_copy(0, far_end).wait_send()
-        across_copy(1, other).wait_send()
-        near_copy(end).wait_send()
-        for seg in aside:
-            side_copy(2, my_seg, end, seg).wait_send()
-            side_copy(3, my_seg, me, seg).wait_send()
+        all_of(others, share_send, share_recv).wait_send()
+        all_of(strain_ref, block_send, other_recv).wait_send()
+        all_of(held.at[end], pass_send, other_recv).wait_send()
+        rows_of(1 + len(aside)).wait_recv()
+        give_out(mine[4], mine[1], mine[3])
+        rows_of(5 + 2 * len(aside)).wait_send()
 
 
 def line(
     banks, segs, chunks,
-    strain_hbm, tpl_hbm, bins_ref, first_hbm, last_hbm, twist_hbm, turn_hbm,
+    strain_hbm, tpl_hbm, bins_ref, first_hbm, last_hbm, spin_hbm,
     out_ref,
-    strain_ref, tpl_ref, held, tpl_re, tpl_im, work, first, last, twist, turn,
+    strain_ref, tpl_ref, held, tpl_re, tpl_im, work, first, last, spin,
     row_bank, row_seg,
     input_sem, table_sem, right_sem, left_sem, recv_sem, bank_send, bank_recv, seg_send, seg_recv,
 ):
@@ -411,7 +366,7 @@
     loads = [
         pltpu.make_async_copy(source, target, table_sem.at[i])
         for i, (source, target) in enumerate(
-            ((first_hbm, first), (twist_hbm, twist), (turn_hbm, turn), (last_hbm, last))
+            ((first_hbm, first), (spin_hbm, spin), (last_hbm, last))
         )
     ]
     for load in loads:
@@ -455,7 +410,7 @@
         s_im = work[pl.ds(1, rows, stride=2), :]
         h_re, h_im = tpl_re[...], tpl_im[...]
         q_re, q_im = h_re * s_re + h_im * s_im, h_re * s_im - h_im * s_re
-        return jnp.sqrt(transform(q_re, q_im, first, last, twist, turn)) / sigma
+        return jnp.sqrt(transform(q_re, q_im, first, last, spin)) / sigma
 
     lane = lax.broadcasted_iota(jnp.int32, (8, LANES), 1)
     row_bank[me] = jnp.zeros((8, LANES), jnp.float32)
@@ -529,7 +484,7 @@
     count, _, width = strain.shape
     length = templates.shape[2]
     depth, rows = width // LANES, length // LANES
-    first, last, twist, turn = tables(length)
+    first, last, spin = tables(length)
     strain = strain.reshape(count, 2, depth, LANES).transpose(0, 2, 1, 3).reshape(count, 2 * depth, LANES)
     tpl = templates.reshape(2, rows, LANES).transpose(1, 0, 2).reshape(2 * rows, LANES)
     vmem = pl.BlockSpec(memory_space=pltpu.VMEM)
@@ -537,7 +492,7 @@
     dma = pltpu.SemaphoreType.DMA
     bf16, f32 = jnp.bfloat16, jnp.float32
     held = pltpu.VMEM((banks, count, 2 * depth, LANES), bf16)
-    constants = [pltpu.VMEM(table.shape, table.dtype) for table in (first, last, twist, turn)]
+    constants = [pltpu.VMEM(table.shape, table.dtype) for table in (first, last, spin)]
     if banks == 4 and count > 2:
         body = functools.partial(middle, banks, segs)
         piece_rows = 2 * rows // segs
@@ -554,25 +509,21 @@
             pltpu.VMEM((3, 2 * rows, LANES), f32),
             *constants,
             pltpu.VMEM((5, 1, LANES), f32),
-            pltpu.VMEM((3, 1, LANES), f32),
-            pltpu.VMEM((segs, 1, LANES), f32),
-            pltpu.VMEM((1, LANES), f32),
+            pltpu.VMEM((max(4, segs + 1) + 2 * segs, 1, LANES), f32),
+            dma,
+            dma,
+            dma((3,)),
+            dma,
+            dma,
             dma((count,)),
-            dma((2,)),
-            dma((4,)),
-            dma((count, PARTS)),
-            dma((count, PARTS)),
-            dma((count, PARTS)),
-            dma((banks, count, PARTS)),
-            dma((1,)),
-            dma((segs,)),
-            dma((segs,)),
-            dma((1,)),
-            dma((1,)),
-            dma((2, segs)),
-            dma((segs,)),
-            dma((2,)),
-            dma((1,)),
+            dma,
+            dma((count // 2 + 1,)),
+            dma,
+            dma,
+            dma,
+            dma,
+            dma,
+            dma,
             pltpu.SemaphoreType.REGULAR,
         ]
     else:
@@ -589,7 +540,7 @@
             pltpu.VMEM((banks, 8, LANES), f32),
             pltpu.VMEM((segs, 8, LANES), f32),
             dma((chunks + 1,)),
-            dma((4,)),
+            dma((3,)),
             dma((banks, chunks)),
             dma((banks, chunks)),
             dma((banks, chunks)),
@@ -601,12 +552,12 @@
     out = pl.pallas_call(
         body,
         out_shape=jax.ShapeDtypeStruct((8, LANES), f32),
-        in_specs=[hbm, hbm, vmem, hbm, hbm, hbm, hbm],
+        in_specs=[hbm, hbm, vmem, hbm, hbm, hbm],
         out_specs=vmem,
         scratch_shapes=scratch,
         compiler_params=pltpu.CompilerParams(collective_id=0, has_side_effects=True, vmem_limit_bytes=GRANT),
         name="search",
-    )(strain, tpl, length_bins.reshape(1, 1), first, last, twist, turn)
+    )(strain, tpl, length_bins.reshape(1, 1), first, last, spin)
     return pl.pallas_call(
         unpack,
         out_shape=[

time: 19.4 us -> 19 us (0.979)
  Pallas kernels: 17.9 us -> 17.6 us
    pallas_call x1, Pallas kernels: 17.4 us -> 17 us  [per_device(): pl.pallas_call(body, out_shape=jax.ShapeDtypeStruct((8, LANES), f32), in_...]
where the time goes in v4:
time: 19 us; the launch traced here: 18.8 us
  Pallas kernels  17.6 us (93%)
  between operations  1.28 us (7%)
    pallas_call x1, Pallas kernels, per_device(): pl.pallas_call(body, out_shape=jax.ShapeDtypeStruct((8, LANES), f32), in_...  17 us
    pallas_call x1, Pallas kernels, per_device(): pl.pallas_call(unpack, out_shape=[jax.ShapeDtypeStruct((1, count), f32),...  0.52 us

profile of v4, /device:TPU:0, one launch (start us, length us, event | category | flops | bytes accessed | tf_op | source)
XLA Modules:
  0.0 18.8 jit_solution(7265627133173230109)
XLA Ops:
  1.3 17.0 %search.1.out_ref = f32[8,128]{1,0:T(8,128)S(1)} custom-call(bf16[4,128,128]{2,1,0:T(8,128)(2,1)} %bitcast.12, bf16[512,128]{1,0:T(8,128)(2,1)} %bitcast.13, s32[1,1]{1,0:T(1,128)} %bitcast.11.bins_ref, bf16[128,384]{1,0:T(8,128)(2,1)} %constant.6.clone.first_hbm, bf16[768,256]{1,0:T(8,128)(2,1)} %constant.7.clone.last_hbm, ...), custom_call_target="tpu_custom_call" | custom-call | tf_op jit(solution)/shard_map/search/pallas_call | solution.py:552
  18.3 0.5 %unpack.1 = (f32[1,4]{1,0:T(1,128)}, f32[4]{0:T(128)}, f32[1]{0:T(128)}) custom-call(f32[8,128]{1,0:T(8,128)S(1)} %search.1.out_ref), custom_call_target="tpu_custom_call" | custom-call | tf_op jit(solution)/shard_map/unpack/pallas_call | solution.py:561

commit v5 on v4

--- a/solution.py
+++ b/solution.py
@@ -56,14 +56,29 @@
     return a[0] * b[0] - a[1] * b[1], a[0] * b[1] + a[1] * b[0]
 
 
+def butterfly(parts):
+    number = len(parts)
+    if number == 1:
+        return parts
+    evens, odds = butterfly(parts[0::2]), butterfly(parts[1::2])
+    root = math.sqrt(0.5)
+    out = [None] * number
+    for way, ((a, b), (c, d)) in enumerate(zip(evens, odds)):
+        if 4 * way == number:
+            c, d = -d, c
+        elif 8 * way == number:
+            c, d = (c - d) * root, (c + d) * root
+        elif 8 * way == 3 * number:
+            c, d = (c + d) * -root, (c - d) * root
+        out[way], out[way + number // 2] = (a + c, b + d), (a - c, b - d)
+    return out
+
+
 def transform(q_re, q_im, first, last, spin):
     depth = q_re.shape[0] // WAYS
-    (a, e), (b, f), (c, g), (d, h) = [
-        (q_re[depth * i : depth * (i + 1)], q_im[depth * i : depth * (i + 1)]) for i in range(WAYS)
-    ]
-    p_re, p_im, m_re, m_im = a + c, e + g, a - c, e - g
-    r_re, r_im, n_re, n_im = b + d, f + h, b - d, f - h
-    ways = [(p_re + r_re, p_im + r_im), (m_re - n_im, m_im + n_re), (p_re - r_re, p_im - r_im), (m_re + n_im, m_im - n_re)]
+    ways = butterfly(
+        [(q_re[depth * i : depth * (i + 1)], q_im[depth * i : depth * (i + 1)]) for i in range(WAYS)]
+    )
     ways = ways[:1] + [times(ways[i], (spin[WAYS + i - 1, 0], spin[WAYS + i - 1, 1])) for i in range(1, WAYS)]
     y = jnp.concatenate([jnp.concatenate([way[i] for way in ways], axis=1) for i in (0, 1)], axis=0)
     high, low = split(y)
@@ -91,6 +106,7 @@
     my_seg = lax.axis_index("seg")
     count = strain_ref.shape[0]
     rows = tpl_ref.shape[0] // 2
+    depth = strain_ref.shape[1] // 2
     piece_rows = lent.shape[1]
     is_end = (me == 0) | (me == banks - 1)
     is_hub = jnp.logical_not(is_end)
@@ -205,12 +221,18 @@
         rows_of(4 + len(aside)).wait_recv()
         give_out(inbox[near], inbox[near + 1], inbox[near + 2])
 
-    def deinterleave(value, slot):
-        work[slot] = value
-        return work[slot, pl.ds(0, rows, stride=2), :], work[slot, pl.ds(1, rows, stride=2), :]
+    def place(block, origin, chunk):
+        spare = work.at[2 + chunk]
+        spare[pl.ds(origin * (2 * depth), 2 * depth), :] = block.astype(jnp.float32)
+        part = pl.ds(pl.multiple_of(origin * depth, depth), depth)
+        for i, target in enumerate((s_re, s_im)):
+            target[chunk, part, :] = spare[pl.ds(origin * (2 * depth) + i, depth, stride=2), :]
 
     def prepare(slot, value):
-        h_re[slot], h_im[slot] = deinterleave(value, 2)
+        spare = work.at[slot]
+        spare[...] = value
+        for i, target in enumerate((h_re, h_im)):
+            target[slot] = spare[pl.ds(i, rows, stride=2), :]
         return jnp.sqrt(jnp.sum(value * value, keepdims=True) + EPSILON)
 
     def peak(slot, seg):
@@ -229,7 +251,6 @@
         sigma = prepare(0, mask(tpl_ref[...], 0))
         for load in loads:
             load.wait()
-        held[me] = strain_ref[...]
         for chunk in range(count):
             @pl.when(end == lender(chunk))
             def _():
@@ -241,15 +262,18 @@
             passed(end, chunk, other).start()
         all_of(held.at[other], block_send, other_recv).wait_recv()
 
+        for chunk in range(count):
+            place(strain_ref[chunk], me, chunk)
+            for origin in (end, other):
+                place(held[origin, chunk], origin, chunk)
+
         def gather(*chunks):
             if len(chunks) > 1:
                 all_of(held.at[far_end, pl.ds(chunks[0], len(chunks))], pass_send, far_recv.at[chunks[0]]).wait_recv()
             else:
                 passed(far_end, chunks[0], me).wait_recv()
             for chunk in chunks:
-                s_re[chunk], s_im[chunk] = deinterleave(
-                    held[:, chunk].reshape(2 * rows, LANES).astype(jnp.float32), chunk % 2
-                )
+                place(held[far_end, chunk], far_end, chunk)
 
         def borrow():
             all_of(others, share_send, share_recv).wait_recv()
@@ -506,7 +530,7 @@
             pltpu.VMEM((2, rows, LANES), f32),
             pltpu.VMEM((count, rows, LANES), f32),
             pltpu.VMEM((count, rows, LANES), f32),
-            pltpu.VMEM((3, 2 * rows, LANES), f32),
+            pltpu.VMEM((2 + count, 2 * rows, LANES), f32),
             *constants,
             pltpu.VMEM((5, 1, LANES), f32),
             pltpu.VMEM((max(4, segs + 1) + 2 * segs, 1, LANES), f32),

time: 19 us -> 19 us (level)
  no operation moved by 1% of the time
where the time goes in v5:
time: 19 us; the launch traced here: 18.8 us
  Pallas kernels  17.5 us (92%)
  between operations  1.28 us (7%)
    pallas_call x1, Pallas kernels, per_device(): pl.pallas_call(body, out_shape=jax.ShapeDtypeStruct((8, LANES), f32), in_...  17 us
    pallas_call x1, Pallas kernels, per_device(): pl.pallas_call(unpack, out_shape=[jax.ShapeDtypeStruct((1, count), f32),...  0.52 us

profile of v5, /device:TPU:0, one launch (start us, length us, event | category | flops | bytes accessed | tf_op | source)
XLA Modules:
  0.0 18.8 jit_solution(7486084569715570789)
XLA Ops:
  1.3 17.0 %search.1.out_ref = f32[8,128]{1,0:T(8,128)S(1)} custom-call(bf16[4,128,128]{2,1,0:T(8,128)(2,1)} %bitcast.12, bf16[512,128]{1,0:T(8,128)(2,1)} %bitcast.13, s32[1,1]{1,0:T(1,128)} %bitcast.11.bins_ref, bf16[128,384]{1,0:T(8,128)(2,1)} %constant.6.clone.first_hbm, bf16[768,256]{1,0:T(8,128)(2,1)} %constant.7.clone.last_hbm, ...), custom_call_target="tpu_custom_call" | custom-call | tf_op jit(solution)/shard_map/search/pallas_call | solution.py:576
  18.3 0.5 %unpack.1 = (f32[1,4]{1,0:T(1,128)}, f32[4]{0:T(128)}, f32[1]{0:T(128)}) custom-call(f32[8,128]{1,0:T(8,128)S(1)} %search.1.out_ref), custom_call_target="tpu_custom_call" | custom-call | tf_op jit(solution)/shard_map/unpack/pallas_call | solution.py:585

commit v6 on v5

--- a/solution.py
+++ b/solution.py
@@ -12,8 +12,8 @@
 MESH = pl.DeviceIdType.MESH
 EPSILON = 1e-06
 LANES = 128
-WAYS = 4
-GRANT = 56492032
+WAYS = 8
+GRANT = 56549376
 
 
 def split(value):
@@ -237,7 +237,7 @@
 
     def peak(slot, seg):
         a, b, c, d = s_re[seg], s_im[seg], h_re[slot], h_im[slot]
-        return jnp.sqrt(transform(c * a + d * b, c * b - d * a, first, last, spin))
+        return transform(c * a + d * b, c * b - d * a, first, last, spin)
 
     @pl.when(is_hub)
     def _():
@@ -284,9 +284,9 @@
         def row(values, scale):
             out, most = jnp.zeros((1, LANES), jnp.float32), values[0]
             for chunk in range(count):
-                out = jnp.where(lane == chunk, values[chunk] / scale, out)
+                out = jnp.where(lane == chunk, values[chunk], out)
                 most = jnp.maximum(most, values[chunk])
-            return out, jnp.broadcast_to(most / scale, (1, LANES))
+            return jnp.sqrt(out) / scale, jnp.sqrt(jnp.broadcast_to(most, (1, LANES))) / scale
 
         def send_side(sigma_two):
             mine[0], mine[2] = row(theirs, sigma_two)

time: 19 us -> 18.9 us (level)
  no operation moved by 1% of the time
where the time goes in v6:
time: 18.9 us; the launch traced here: 18.7 us
  Pallas kernels  17.5 us (93%)
  between operations  1.28 us (7%)
    pallas_call x1, Pallas kernels, per_device(): pl.pallas_call(body, out_shape=jax.ShapeDtypeStruct((8, LANES), f32), in_...  16.9 us
    pallas_call x1, Pallas kernels, per_device(): pl.pallas_call(unpack, out_shape=[jax.ShapeDtypeStruct((1, count), f32),...  0.52 us

profile of v6, /device:TPU:0, one launch (start us, length us, event | category | flops | bytes accessed | tf_op | source)
XLA Modules:
  0.0 18.7 jit_solution(12757452629352614006)
XLA Ops:
  1.3 16.9 %search.1.out_ref = f32[8,128]{1,0:T(8,128)S(1)} custom-call(bf16[4,128,128]{2,1,0:T(8,128)(2,1)} %bitcast.12, bf16[512,128]{1,0:T(8,128)(2,1)} %bitcast.13, s32[1,1]{1,0:T(1,128)} %bitcast.11.bins_ref, bf16[64,192]{1,0:T(8,128)(2,1)} %constant.6.clone.first_hbm, bf16[768,256]{1,0:T(8,128)(2,1)} %constant.7.clone.last_hbm, ...), custom_call_target="tpu_custom_call" | custom-call | tf_op jit(solution)/shard_map/search/pallas_call | solution.py:576
  18.2 0.5 %unpack.1 = (f32[1,4]{1,0:T(1,128)}, f32[4]{0:T(128)}, f32[1]{0:T(128)}) custom-call(f32[8,128]{1,0:T(8,128)S(1)} %search.1.out_ref), custom_call_target="tpu_custom_call" | custom-call | tf_op jit(solution)/shard_map/unpack/pallas_call | solution.py:585
